TPU v7x, 32 devices: a whole 2x2x4 slice. The times are simulated.
32 devices in a mesh: shard: 4 (over x, core), ctx: 2 (over y), tp: 4 (over z).
Axes of the slice: x: 2, y: 2, z: 4, core: 2. Of those that a mesh axis runs over, the one named last changes fastest.
Arguments:
- tokens: bfloat16 [8192, 1024], P(('shard', 'ctx')), may hold values from -6 to 6
- segment_ids: int32 [8192], P('shard'), may hold values from -1 to 3, as said below
- cotangent: bfloat16 [8192, 1024], P(('shard', 'ctx')), may hold values from -6 to 6
- norm_gain: bfloat16 [1024], P('shard'), may hold values from 0.5 to 1.5
- w_query: bfloat16 [1024, 1024], P('shard', 'tp'), may hold values from -0.1875 to 0.1875
- w_key: bfloat16 [1024, 1024], P('shard', 'tp'), may hold values from -0.1875 to 0.1875
- w_value: bfloat16 [1024, 2048], P('shard', 'tp'), may hold values from -0.1875 to 0.1875
- w_outgate: bfloat16 [1024, 2048], P('shard', 'tp'), may hold values from -0.1875 to 0.1875
- w_beta: bfloat16 [1024, 8], P('shard', 'tp'), may hold values from -0.1875 to 0.1875
- w_decay: bfloat16 [1024, 8], P('shard', 'tp'), may hold values from -0.1875 to 0.1875
- decay_bias: bfloat16 [8], P('tp'), may hold values from -8 to -2.5
- conv_query: bfloat16 [4, 8, 128], P(None, 'tp', 'shard'), may hold values from -3 to 3
- conv_key: bfloat16 [4, 8, 128], P(None, 'tp', 'shard'), may hold values from -3 to 3
- conv_value: bfloat16 [4, 8, 256], P(None, 'tp', 'shard'), may hold values from -3 to 3
- out_gain: bfloat16 [8, 256], P('tp', 'shard'), may hold values from 0.5 to 1.5
- w_out: bfloat16 [2048, 1024], P('tp', 'shard'), may hold values from -0.125 to 0.125
- mlp_gain: bfloat16 [1024], P('shard'), may hold values from 0.5 to 1.5
- w_gate: bfloat16 [1024, 2816], P('shard', 'tp'), may hold values from -0.1875 to 0.1875
- w_up: bfloat16 [1024, 2816], P('shard', 'tp'), may hold values from -0.1875 to 0.1875
- w_down: bfloat16 [2816, 1024], P('tp', 'shard'), may hold values from -0.109375 to 0.109375
Outputs:
- output: bfloat16 [8192, 1024], P(('shard', 'ctx'))
- input_grad: float32 [8192, 1024], P(('shard', 'ctx'))
- norm_gain_grad: float32 [1024], P('shard')
- w_query_grad: float32 [1024, 1024], P('shard', 'tp')
- w_key_grad: float32 [1024, 1024], P('shard', 'tp')
- w_value_grad: float32 [1024, 2048], P('shard', 'tp')
- w_outgate_grad: float32 [1024, 2048], P('shard', 'tp')
- w_beta_grad: float32 [1024, 8], P('shard', 'tp')
- w_decay_grad: float32 [1024, 8], P('shard', 'tp')
- decay_bias_grad: float32 [8], P('tp')
- conv_query_grad: float32 [4, 8, 128], P(None, 'tp', 'shard')
- conv_key_grad: float32 [4, 8, 128], P(None, 'tp', 'shard')
- conv_value_grad: float32 [4, 8, 256], P(None, 'tp', 'shard')
- out_gain_grad: float32 [8, 256], P('tp', 'shard')
- w_out_grad: float32 [2048, 1024], P('tp', 'shard')
- mlp_gain_grad: float32 [1024], P('shard')
- w_gate_grad: float32 [1024, 2816], P('shard', 'tp')
- w_up_grad: float32 [1024, 2816], P('shard', 'tp')
- w_down_grad: float32 [2816, 1024], P('tp', 'shard')
Inputs may be any that keep to these rules, and one draw needn't show every extreme that they name: `segment_ids`: within each aligned block of 2048 slots (one block a pack), the live slots come first and number between 1280 and 1792; the remaining slots are padding with id -1. Over the live slots ids never fall, and equal ids form one sequence; a pack holds one to four sequences, exactly one of them has 1024 slots, all others fewer, and the last live slot of every pack has id 3.
All inputs are finite; a program needn't handle non-finite values.
Results may differ from a plain program's by a relative error of at most 0.025.
Values may be sent and summed in bfloat16 or wider, within the bound.
A program may use at most 192 MiB of HBM per device.

v0:
```python
from functools import partial

import jax
import jax.numpy as jnp
from jax import lax
from jax.sharding import PartitionSpec as P

BLOCK = 64


EPSILON = 1e-06


def matmul(left, right):
    return jnp.dot(left, right, precision=lax.Precision.HIGHEST)


def dot_plain(left, right):
    return jnp.dot(left, right, preferred_element_type=jnp.float32)


def dot_back(left, right):
    return lax.dot_general(
        left, right, (((1,), (1,)), ((), ())), preferred_element_type=jnp.float32
    )


def dot_outer(left, right):
    return lax.dot_general(
        left, right, (((0,), (0,)), ((), ())), preferred_element_type=jnp.float32
    )


def rms_norm(vector, scale_gain):
    return (
        vector * lax.rsqrt(jnp.mean(vector * vector, axis=-1, keepdims=True) + EPSILON) * scale_gain
    )


def unit_rows(vector):
    return vector * lax.rsqrt(jnp.sum(vector * vector, axis=-1, keepdims=True) + EPSILON)


def short_conv(signal, kernel, segments):
    result = signal * kernel[0]
    for offset in range(1, kernel.shape[0]):
        shifted = jnp.concatenate(
            [jnp.zeros((offset, signal.shape[1]), signal.dtype), signal[:-offset]], axis=0
        )
        earlier = jnp.concatenate([jnp.full((offset,), -2, jnp.int32), segments[:-offset]], axis=0)
        result = result + jnp.where((earlier == segments)[:, None], shifted, 0.0) * kernel[offset]
    return result


def delta_block(carry_state, pieces):
    query_rows, key_rows, value_rows, beta_rows, decay_rows, seg_rows, before = pieces
    block_span = query_rows.shape[0]
    row_index = lax.broadcasted_iota(jnp.int32, (block_span, block_span), 0)
    col_index = lax.broadcasted_iota(jnp.int32, (block_span, block_span), 1)
    below_diag = row_index >= col_index
    cumulative = jnp.cumsum(decay_rows)
    inside = below_diag & (seg_rows[:, None] == seg_rows[None, :])
    spread = jnp.where(below_diag, cumulative[:, None] - cumulative[None, :], 0.0)
    fading = jnp.where(inside, jnp.exp(spread), 0.0)
    carried = jnp.where(seg_rows == before, jnp.exp(cumulative), 0.0)
    intersection = matmul(key_rows, key_rows.T)
    strict = jnp.where(row_index > col_index, beta_rows[:, None] * fading * intersection, 0.0)
    system = strict + jnp.eye(block_span, dtype=carry_state.dtype)
    target = beta_rows[:, None] * (value_rows - carried[:, None] * matmul(key_rows, carry_state))
    update = jax.scipy.linalg.solve_triangular(system, target, lower=True, unit_diagonal=True)
    scores = fading * matmul(query_rows, key_rows.T)
    output = carried[:, None] * matmul(query_rows, carry_state) + matmul(scores, update)
    next_state = carried[-1] * carry_state + matmul(key_rows.T, fading[-1][:, None] * update)
    return (next_state, output)


def delta_rule(queries, keys_in, values, beta_rows, decay_rows, segments):
    block_count = queries.shape[0] // BLOCK
    before = jnp.concatenate([jnp.full((1,), -2, jnp.int32), segments[:-1]], axis=0)
    before = before.reshape(block_count, BLOCK)[:, 0]
    pieces = (
        queries.reshape(block_count, BLOCK, -1),
        keys_in.reshape(block_count, BLOCK, -1),
        values.reshape(block_count, BLOCK, -1),
        beta_rows.reshape(block_count, BLOCK),
        decay_rows.reshape(block_count, BLOCK),
        segments.reshape(block_count, BLOCK),
        before,
    )
    start_state = jnp.zeros((queries.shape[1], values.shape[1]), jnp.float32)
    ignored, outputs = lax.scan(jax.checkpoint(delta_block), start_state, pieces)
    return outputs.reshape(queries.shape[0], values.shape[1])


def mixer_columns(
    seg_all, query_head, key_head, value_cols, beta_head, decay_head, taps_q, taps_k, taps_v
):
    queries = unit_rows(jax.nn.silu(short_conv(query_head, taps_q, seg_all))) * query_head.shape[
        1
    ] ** (-0.5)
    keys_in = unit_rows(jax.nn.silu(short_conv(key_head, taps_k, seg_all)))
    values = jax.nn.silu(short_conv(value_cols, taps_v, seg_all))
    return delta_rule(queries, keys_in, values, beta_head, decay_head, seg_all)


def gated_norm(mixed_in, gate_in, gain_in, live_rows):
    head_count = gain_in.shape[0]
    per_head = mixed_in.reshape(mixed_in.shape[0], head_count, -1)
    gated_rows = rms_norm(per_head, gain_in) * jax.nn.silu(gate_in).reshape(per_head.shape)
    return (gated_rows * live_rows[:, None, None]).reshape(mixed_in.shape)


def gate_rates(beta_lin, decay_lin, bias_in):
    return (jax.nn.sigmoid(beta_lin), -jax.nn.softplus(decay_lin + bias_in))


def shards(
    tokens,
    segment_ids,
    cotangent,
    norm_gain,
    w_query,
    w_key,
    w_value,
    w_outgate,
    w_beta,
    w_decay,
    decay_bias,
    conv_query,
    conv_key,
    conv_value,
    out_gain,
    w_out,
    mlp_gain,
    w_gate,
    w_up,
    w_down,
):
    (
        gain_one,
        query_w,
        key_w,
        value_w,
        outgate_w,
        beta_w,
        decay_w,
        taps_query,
        taps_key,
        taps_value,
        head_gain,
        out_w,
        gain_two,
        gate_w,
        up_w,
        down_w,
    ) = (
        lax.all_gather(norm_gain, "shard", axis=0, tiled=True),
        lax.all_gather(w_query, "shard", axis=0, tiled=True),
        lax.all_gather(w_key, "shard", axis=0, tiled=True),
        lax.all_gather(w_value, "shard", axis=0, tiled=True),
        lax.all_gather(w_outgate, "shard", axis=0, tiled=True),
        lax.all_gather(w_beta, "shard", axis=0, tiled=True),
        lax.all_gather(w_decay, "shard", axis=0, tiled=True),
        lax.all_gather(conv_query, "shard", axis=2, tiled=True),
        lax.all_gather(conv_key, "shard", axis=2, tiled=True),
        lax.all_gather(conv_value, "shard", axis=2, tiled=True),
        lax.all_gather(out_gain, "shard", axis=1, tiled=True),
        lax.all_gather(w_out, "shard", axis=1, tiled=True),
        lax.all_gather(mlp_gain, "shard", axis=0, tiled=True),
        lax.all_gather(w_gate, "shard", axis=0, tiled=True),
        lax.all_gather(w_up, "shard", axis=0, tiled=True),
        lax.all_gather(w_down, "shard", axis=1, tiled=True),
    )
    ctx_size = lax.axis_size("ctx")
    ctx_rank = lax.axis_index("ctx")
    rows_here = tokens.shape[0]
    heads_here = decay_bias.shape[0]
    conv_taps = taps_query.shape[0]
    key_size = taps_query.shape[2]
    value_size = head_gain.shape[1]
    col_width = heads_here * value_size // ctx_size
    my_head = ctx_rank * col_width // value_size
    my_first = ctx_rank * col_width
    run_ids = lax.dynamic_slice_in_dim(segment_ids, ctx_rank * rows_here, rows_here)
    live_rows = (run_ids >= 0).astype(jnp.float32)
    inputs32 = tokens.astype(jnp.float32)
    normed32, norm_one_back = jax.vjp(rms_norm, inputs32, gain_one.astype(jnp.float32))
    normed = normed32.astype(jnp.bfloat16)
    query_raw = dot_plain(normed, query_w).astype(jnp.bfloat16)
    key_raw = dot_plain(normed, key_w).astype(jnp.bfloat16)
    value_raw = dot_plain(normed, value_w).astype(jnp.bfloat16)
    gate_raw = dot_plain(normed, outgate_w)
    small_w = jnp.concatenate([beta_w, decay_w], axis=1)
    small_lin = dot_plain(normed, small_w)
    (beta_rows, decays), rates_back = jax.vjp(
        gate_rates,
        small_lin[:, :heads_here],
        small_lin[:, heads_here:],
        decay_bias.astype(jnp.float32),
    )
    query_all, key_all, beta_all, decay_all = (
        lax.all_gather(query_raw, "ctx", axis=0, tiled=True),
        lax.all_gather(key_raw, "ctx", axis=0, tiled=True),
        lax.all_gather(beta_rows.astype(jnp.bfloat16), "ctx", axis=0, tiled=True),
        lax.all_gather(decays.astype(jnp.bfloat16), "ctx", axis=0, tiled=True),
    )
    value_cols = lax.all_to_all(value_raw, "ctx", split_axis=1, concat_axis=0, tiled=True)
    query_head = lax.dynamic_slice_in_dim(query_all, my_head * key_size, key_size, 1).astype(
        jnp.float32
    )
    key_head = lax.dynamic_slice_in_dim(key_all, my_head * key_size, key_size, 1).astype(
        jnp.float32
    )
    beta_head = lax.dynamic_slice_in_dim(beta_all, my_head, 1, 1)[:, 0].astype(jnp.float32)
    decay_head = lax.dynamic_slice_in_dim(decay_all, my_head, 1, 1)[:, 0].astype(jnp.float32)
    taps_q = lax.dynamic_index_in_dim(taps_query, my_head, 1, keepdims=False).astype(jnp.float32)
    taps_k = lax.dynamic_index_in_dim(taps_key, my_head, 1, keepdims=False).astype(jnp.float32)
    taps_v = lax.dynamic_slice_in_dim(
        taps_value.reshape(conv_taps, -1), my_first, col_width, 1
    ).astype(jnp.float32)
    mixed_cols, mixer_back = jax.vjp(
        partial(mixer_columns, segment_ids),
        query_head,
        key_head,
        value_cols.astype(jnp.float32),
        beta_head,
        decay_head,
        taps_q,
        taps_k,
        taps_v,
    )
    mixed_rows = lax.all_to_all(
        mixed_cols.astype(jnp.bfloat16), "ctx", split_axis=0, concat_axis=1, tiled=True
    )
    gated32, gated_back = jax.vjp(
        lambda mixed_in, gate_in, gain_in: gated_norm(mixed_in, gate_in, gain_in, live_rows),
        mixed_rows.astype(jnp.float32),
        gate_raw,
        head_gain.astype(jnp.float32),
    )
    gated_rows = gated32.astype(jnp.bfloat16)
    attended = lax.psum(dot_plain(gated_rows, out_w), "tp")
    hidden_in = inputs32 + attended
    normed_two32, norm_two_back = jax.vjp(rms_norm, hidden_in, gain_two.astype(jnp.float32))
    normed_two = normed_two32.astype(jnp.bfloat16)
    gate_two = dot_plain(normed_two, gate_w)
    up_two = dot_plain(normed_two, up_w)
    sigmoid_two = jax.nn.sigmoid(gate_two)
    activated = gate_two * sigmoid_two
    hidden = (activated * up_two).astype(jnp.bfloat16)
    mlp_out = lax.psum(dot_plain(hidden, down_w).astype(jnp.bfloat16), "tp").astype(jnp.float32)
    result = (hidden_in + mlp_out).astype(jnp.bfloat16)
    grad_hidden = dot_back(cotangent, down_w)
    gate_slope = sigmoid_two * (1.0 + gate_two * (1.0 - sigmoid_two))
    grad_gate = (grad_hidden * up_two * gate_slope).astype(jnp.bfloat16)
    grad_up = (grad_hidden * activated).astype(jnp.bfloat16)
    grad_down_w = dot_outer(hidden, cotangent)
    grad_gate_w = dot_outer(normed_two, grad_gate)
    grad_up_w = dot_outer(normed_two, grad_up)
    grad_normed_two = lax.psum(dot_back(grad_gate, gate_w) + dot_back(grad_up, up_w), "tp")
    grad_hidden_in, grad_gain_two = norm_two_back(grad_normed_two)
    grad_hidden_in = grad_hidden_in + cotangent.astype(jnp.float32)
    grad_branch = grad_hidden_in.astype(jnp.bfloat16)
    grad_out_w = dot_outer(gated_rows, grad_branch)
    grad_gated = dot_back(grad_branch, out_w)
    grad_mixed, grad_gate_raw, grad_head_gain = gated_back(grad_gated)
    grad_cols = lax.all_to_all(
        grad_mixed.astype(jnp.bfloat16), "ctx", split_axis=1, concat_axis=0, tiled=True
    )
    (
        grad_query_head,
        grad_key_head,
        grad_value_cols,
        grad_beta_head,
        grad_decay_head,
        grad_taps_q,
        grad_taps_k,
        grad_taps_v,
    ) = mixer_back(grad_cols.astype(jnp.float32))
    back_query, back_key, back_beta, back_decay, back_value = (
        lax.all_to_all(
            grad_query_head.astype(jnp.bfloat16), "ctx", split_axis=0, concat_axis=1, tiled=True
        ).astype(grad_query_head.dtype),
        lax.all_to_all(
            grad_key_head.astype(jnp.bfloat16), "ctx", split_axis=0, concat_axis=1, tiled=True
        ).astype(grad_key_head.dtype),
        lax.all_to_all(
            grad_beta_head[:, None].astype(jnp.bfloat16),
            "ctx",
            split_axis=0,
            concat_axis=1,
            tiled=True,
        ).astype(jnp.float32),
        lax.all_to_all(
            grad_decay_head[:, None].astype(jnp.bfloat16),
            "ctx",
            split_axis=0,
            concat_axis=1,
            tiled=True,
        ).astype(jnp.float32),
        lax.all_to_all(
            grad_value_cols.astype(jnp.bfloat16), "ctx", split_axis=0, concat_axis=1, tiled=True
        ).astype(grad_value_cols.dtype),
    )
    devices_per_head = ctx_size // heads_here
    grad_query = back_query.reshape(rows_here, heads_here, devices_per_head, key_size).sum(axis=2)
    grad_query = grad_query.reshape(rows_here, heads_here * key_size).astype(jnp.bfloat16)
    grad_key = back_key.reshape(rows_here, heads_here, devices_per_head, key_size).sum(axis=2)
    grad_key = grad_key.reshape(rows_here, heads_here * key_size).astype(jnp.bfloat16)
    grad_beta = back_beta.reshape(rows_here, heads_here, devices_per_head).sum(axis=2)
    grad_decay = back_decay.reshape(rows_here, heads_here, devices_per_head).sum(axis=2)
    grad_value = back_value.astype(jnp.bfloat16)
    grad_gate_low = grad_gate_raw.astype(jnp.bfloat16)
    grad_beta_lin, grad_decay_lin, grad_bias = rates_back((grad_beta, grad_decay))
    grad_small = jnp.concatenate([grad_beta_lin, grad_decay_lin], axis=1)
    grad_query_w = dot_outer(normed, grad_query)
    grad_key_w = dot_outer(normed, grad_key)
    grad_value_w = dot_outer(normed, grad_value)
    grad_outgate_w = dot_outer(normed, grad_gate_low)
    grad_small_w = jnp.dot(normed.T, grad_small, precision=lax.Precision.HIGHEST)
    grad_normed_part = (
        dot_back(grad_query, query_w)
        + dot_back(grad_key, key_w)
        + dot_back(grad_value, value_w)
        + dot_back(grad_gate_low, outgate_w)
        + jnp.dot(grad_small, small_w.astype(jnp.float32).T, precision=lax.Precision.HIGHEST)
    )
    grad_normed = lax.psum(grad_normed_part.astype(jnp.bfloat16), "tp").astype(jnp.float32)
    grad_inputs, grad_gain_one = norm_one_back(grad_normed)
    input_grad = grad_inputs + grad_hidden_in
    grad_conv_q = lax.dynamic_update_slice(
        jnp.zeros((conv_taps, heads_here, key_size), jnp.float32),
        grad_taps_q[:, None, :],
        (0, my_head, 0),
    )
    grad_conv_k = lax.dynamic_update_slice(
        jnp.zeros((conv_taps, heads_here, key_size), jnp.float32),
        grad_taps_k[:, None, :],
        (0, my_head, 0),
    )
    grad_conv_v = lax.dynamic_update_slice(
        jnp.zeros((conv_taps, heads_here * value_size), jnp.float32), grad_taps_v, (0, my_first)
    ).reshape(conv_taps, heads_here, value_size)
    bias_tiled = jnp.broadcast_to(grad_bias[None, :], (lax.axis_size("shard"), heads_here))
    (
        part_gain_one,
        part_query,
        part_key,
        part_value,
        part_outgate,
        part_beta,
        part_decay,
        part_bias,
        part_conv_q,
        part_conv_k,
        part_conv_v,
        part_head_gain,
        part_out,
        part_gain_two,
        part_gate,
        part_up,
        part_down,
    ) = (
        lax.psum_scatter(grad_gain_one, "shard", scatter_dimension=0, tiled=True),
        lax.psum_scatter(grad_query_w, "shard", scatter_dimension=0, tiled=True),
        lax.psum_scatter(grad_key_w, "shard", scatter_dimension=0, tiled=True),
        lax.psum_scatter(grad_value_w, "shard", scatter_dimension=0, tiled=True),
        lax.psum_scatter(grad_outgate_w, "shard", scatter_dimension=0, tiled=True),
        lax.psum_scatter(grad_small_w[:, :heads_here], "shard", scatter_dimension=0, tiled=True),
        lax.psum_scatter(grad_small_w[:, heads_here:], "shard", scatter_dimension=0, tiled=True),
        lax.psum_scatter(bias_tiled, "shard", scatter_dimension=0, tiled=True),
        lax.psum_scatter(grad_conv_q, "shard", scatter_dimension=2, tiled=True),
        lax.psum_scatter(grad_conv_k, "shard", scatter_dimension=2, tiled=True),
        lax.psum_scatter(grad_conv_v, "shard", scatter_dimension=2, tiled=True),
        lax.psum_scatter(grad_head_gain, "shard", scatter_dimension=1, tiled=True),
        lax.psum_scatter(grad_out_w, "shard", scatter_dimension=1, tiled=True),
        lax.psum_scatter(grad_gain_two, "shard", scatter_dimension=0, tiled=True),
        lax.psum_scatter(grad_gate_w, "shard", scatter_dimension=0, tiled=True),
        lax.psum_scatter(grad_up_w, "shard", scatter_dimension=0, tiled=True),
        lax.psum_scatter(grad_down_w, "shard", scatter_dimension=1, tiled=True),
    )
    (
        part_gain_one,
        part_query,
        part_key,
        part_value,
        part_outgate,
        part_beta,
        part_decay,
        part_bias,
        part_conv_q,
        part_conv_k,
        part_conv_v,
        part_head_gain,
        part_out,
        part_gain_two,
        part_gate,
        part_up,
        part_down,
    ) = lax.psum(
        (
            part_gain_one,
            part_query,
            part_key,
            part_value,
            part_outgate,
            part_beta,
            part_decay,
            part_bias,
            part_conv_q,
            part_conv_k,
            part_conv_v,
            part_head_gain,
            part_out,
            part_gain_two,
            part_gate,
            part_up,
            part_down,
        ),
        "ctx",
    )
    return (
        result,
        input_grad,
        part_gain_one,
        part_query,
        part_key,
        part_value,
        part_outgate,
        part_beta,
        part_decay,
        part_bias[0],
        part_conv_q,
        part_conv_k,
        part_conv_v,
        part_head_gain,
        part_out,
        part_gain_two,
        part_gate,
        part_up,
        part_down,
    )


def solution(mesh):
    in_specs = (
        P(("shard", "ctx"), None),
        P("shard"),
        P(("shard", "ctx"), None),
        P("shard"),
        P("shard", "tp"),
        P("shard", "tp"),
        P("shard", "tp"),
        P("shard", "tp"),
        P("shard", "tp"),
        P("shard", "tp"),
        P("tp"),
        P(None, "tp", "shard"),
        P(None, "tp", "shard"),
        P(None, "tp", "shard"),
        P("tp", "shard"),
        P("tp", "shard"),
        P("shard"),
        P("shard", "tp"),
        P("shard", "tp"),
        P("tp", "shard"),
    )
    out_specs = (
        P(("shard", "ctx"), None),
        P(("shard", "ctx"), None),
        P("shard"),
        P("shard", "tp"),
        P("shard", "tp"),
        P("shard", "tp"),
        P("shard", "tp"),
        P("shard", "tp"),
        P("shard", "tp"),
        P("tp"),
        P(None, "tp", "shard"),
        P(None, "tp", "shard"),
        P(None, "tp", "shard"),
        P("tp", "shard"),
        P("tp", "shard"),
        P("shard"),
        P("shard", "tp"),
        P("shard", "tp"),
        P("tp", "shard"),
    )
    return jax.shard_map(shards, mesh=mesh, in_specs=in_specs, out_specs=out_specs, check_vma=False)
```

profile of v0, /device:TPU:0, one launch (start us, length us, event | category | flops | bytes accessed | tf_op | source)
XLA Modules:
  0.0 3330.9 jit_solution(10892199163945093741)
XLA Ops:
  15.6 7.7 all_gather.70
  25.7 7.3 all_gather.64
  114.6 13.1 all-to-all-done
  134.5 557.2 %while.44 = (s32[]{:T(128)}, f32[128,256]{1,0:T(8,128)S(1)}, bf16[32,64,256]{2,1,0:T(8,128)(2,1)}, f32[32,128,256]{2,1,0:T(8,128)}, s32[32,64]{1,0:T(8,128)}, /*...) while((s32[]{:T(128)}, f32[128,256]{1,0:T(8,128)S(1)}, ...), condition=%wide.region_5.7_spmd.clone.clone, body=%wide.region_3.6_spmd.clone.clone.sunk | while | flops 113672320 | bytes 1671110 | solution.py:91
  703.8 8.2 all-to-all-done.1
  729.3 147.7 %all-reduce.46.cloned.1.call-done = f32[1024,1024]{1,0:T(8,128)} async-done(((f32[1024,1024]{1,0:T(8,128)}), f32[1024,1024]{1,0:T(8,128)}) %all-reduce.46.cloned.1.call-update) | async-done | bytes 4194320 | tf_op jit(solution)/shard_map/psum | solution.py:242
  884.2 12.4 all-gather.22.cloned.1.call-done
  901.9 15.4 all-gather.24.cloned.1.call-done
  922.6 15.3 all-gather.26.cloned.1.call-done
  937.9 7.6 multiply_convert_fusion.1
  963.1 143.9 %all-reduce.48.cloned.1.call-done = f32[1024,1024]{1,0:T(8,128)} async-done(((f32[1024,1024]{1,0:T(8,128)}), f32[1024,1024]{1,0:T(8,128)}) %all-reduce.48.cloned.1.call-update) | async-done | bytes 4194320 | tf_op jit(solution)/shard_map/psum | solution.py:260
  1154.8 1571.7 %while.43 = (s32[]{:T(128)}, f32[128,256]{1,0:T(8,128)}, f32[32,64,128]{2,1,0:T(8,128)}, f32[32,64,128]{2,1,0:T(8,128)}, f32[32,64,256]{2,1,0:T(8,128)}, /*index...) while((s32[]{:T(128)}, f32[128,256]{1,0:T(8,128)}, ...), condition=%wide.region_24.26_spmd.clone, body=%wide.region_13.25_spmd.clone.sunk | while | flops 306143488 | bytes 6332175 | solution.py:91
  1166.7 6.3 custom-call.25
  1264.8 6.3 custom-call.25
  1313.9 6.3 custom-call.25
  1362.9 6.3 custom-call.25
  2729.4 6.5 multiply_reduce_fusion.19
  2740.2 9.4 all_to_all.110
  2758.1 9.0 all_to_all.111
  2792.7 14.1 all_to_all.112
  2851.9 20.4 reduce-scatter.33.cloned.1.call-done
  2872.3 33.6 %reduce-scatter.31.cloned.1.call-done = f32[256,512]{1,0:T(8,128)} async-done(((f32[1024,512]{1,0:T(8,128)}), f32[256,512]{1,0:T(8,128)}) %reduce-scatter.31.cloned.1.call-update) | async-done | bytes 524304 | tf_op jit(solution)/shard_map/reduce_scatter | solution.py:367
  2907.8 20.8 reduce-scatter.53.cloned.1.call-done
  2929.4 21.0 reduce-scatter.49.cloned.1.call-done
  2951.3 21.1 reduce-scatter.47.cloned.1.call-done
  2973.3 21.8 reduce-scatter.51.cloned.1.call-done
  2996.1 23.8 reduce-scatter.43.cloned.1.call-done
  3020.8 23.6 reduce-scatter.45.cloned.1.call-done
  3045.4 157.0 %all-reduce.52.cloned.1.call-done = (bf16[1024,1024]{1,0:T(8,128)(2,1)}, bf16[1024,1024]{1,0:T(8,128)(2,1)}) async-done(((bf16[1024,1024]{1,0:T(8,128)(2,1)}, bf16[1024,1024]{1,0:T(8,128)(2,1)}), (bf16[1024,1024]{1,0:T(8,128)(2,1)}, bf16[1024,1024]{1,0:T(8,128)(2,1)})) %all-reduce.52.cloned.1.call-update) | async-done | bytes 4194320 | tf_op jit(solution)/shard_map/psum | solution.py:251
  3205.8 11.1 all-reduce.37
  3217.7 9.8 all-reduce.38
  3235.5 78.9 %all-reduce.50.cloned.1.call-done = (f32[256,256]{1,0:T(8,128)}, f32[256,256]{1,0:T(8,128)}, f32[256,512]{1,0:T(8,128)}, f32[256,512]{1,0:T(8,128)}, f32[512,256...) async-done(((f32[256,256]{1,0:T(8,128)}, f32[256,256]{1,0:T(8,128)}, f32[256,512]{1,0:T(8,128)}, f32[256,512]{1,0:T(8,128)}, ...) | async-done | bytes 4259856 | tf_op jit(solution)/shard_map/psum | solution.py:400
  (3041 shorter events, 2420.2 us)
Async XLA Ops:
  7.2 82.4 %all-gather.16.cloned.1.call-start = ((), (), s32[]{:S(2)}) async-start(), calls=%async_computation.24 | async-start | bytes 1572864 | tf_op jit(solution)/shard_map/all_gather | solution.py:202
  25.6 71.0 %all-gather.12.cloned.1.call-start = ((), (), s32[]{:S(2)}) async-start(), calls=%async_computation.22 | async-start | bytes 1572864 | tf_op jit(solution)/shard_map/all_gather | solution.py:203
  35.3 67.6 %all-gather.14.cloned.1.call-start = ((), (), s32[]{:S(2)}) async-start(), calls=%async_computation.23 | async-start | bytes 1310720 | tf_op jit(solution)/shard_map/all_gather | solution.py:160
  36.0 662.4 %all-gather.18.cloned.1.call-start = ((), (), s32[]{:S(2)}) async-start(), calls=%async_computation.25 | async-start | bytes 1310720 | tf_op jit(solution)/shard_map/all_gather | solution.py:161
  36.6 680.2 %all-gather.20.cloned.1.call-start = ((), (), s32[]{:S(2)}) async-start(), calls=%async_computation.26 | async-start | bytes 1310720 | tf_op jit(solution)/shard_map/all_gather | solution.py:168
  89.6 1042.2 %copy-start.52 = (pred[2048]{0:T(1024)(128)(4,1)}, pred[2048]{0:T(1024)(128)(4,1)S(1)}, u32[]{:S(2)}) copy-start(pred[2048]{0:T(1024)(128)(4,1)S(1)} %get-tuple-element.810) | copy-start | bytes 6148
  108.8 19.0 all-to-all-start
  694.0 18.0 all-to-all-start.1
  698.4 178.6 %all-reduce.46.cloned.1.call-start = ((), (), s32[]{:S(2)}) async-start(), calls=%async_computation.27 | async-start | bytes 8388608 | tf_op jit(solution)/shard_map/psum | solution.py:242
  721.7 174.9 %all-gather.22.cloned.1.call-start = ((), (), s32[]{:S(2)}) async-start(), calls=%async_computation.28 | async-start | bytes 1802240 | tf_op jit(solution)/shard_map/all_gather | solution.py:170
  722.5 194.8 %all-gather.24.cloned.1.call-start = ((), (), s32[]{:S(2)}) async-start(), calls=%async_computation.29 | async-start | bytes 1802240 | tf_op jit(solution)/shard_map/all_gather | solution.py:171
  723.2 214.7 %all-gather.26.cloned.1.call-start = ((), (), s32[]{:S(2)}) async-start(), calls=%async_computation.30 | async-start | bytes 1802240 | tf_op jit(solution)/shard_map/all_gather | solution.py:172
  723.9 383.0 %all-reduce.48.cloned.1.call-start = ((), (), s32[]{:S(2)}) async-start(), calls=%async_computation.31 | async-start | bytes 8388608 | tf_op jit(solution)/shard_map/psum | solution.py:260
  951.8 1899.9 %reduce-scatter.37.cloned.1.call-start = ((), (), s32[]{:S(2)}) async-start(), calls=%async_computation.37 | async-start | bytes 3604480 | tf_op jit(solution)/shard_map/reduce_scatter | solution.py:378
  957.2 1894.6 %reduce-scatter.39.cloned.1.call-start = ((), (), s32[]{:S(2)}) async-start(), calls=%async_computation.38 | async-start | bytes 3604480 | tf_op jit(solution)/shard_map/reduce_scatter | solution.py:379
  1126.0 18.0 all-to-all-start.2
  1130.4 1721.4 %reduce-scatter.41.cloned.1.call-start = ((), (), s32[]{:S(2)}) async-start(), calls=%async_computation.39 | async-start | bytes 3604480 | tf_op jit(solution)/shard_map/reduce_scatter | solution.py:380
  1137.8 1714.0 %reduce-scatter.29.cloned.1.call-start = ((), (), s32[]{:S(2)}) async-start(), calls=%async_computation.33 | async-start | bytes 1310720 | tf_op jit(solution)/shard_map/reduce_scatter | solution.py:366
  2753.9 97.9 %reduce-scatter.27.cloned.1.call-start = ((), (), s32[]{:S(2)}) async-start(), calls=%async_computation.32 | async-start | bytes 1310720 | tf_op jit(solution)/shard_map/reduce_scatter | solution.py:365
  2771.5 80.4 %reduce-scatter.35.cloned.1.call-start = ((), (), s32[]{:S(2)}) async-start(), calls=%async_computation.36 | async-start | bytes 2621440 | tf_op jit(solution)/shard_map/reduce_scatter | solution.py:376
  2776.3 96.0 %reduce-scatter.33.cloned.1.call-start = ((), (), s32[]{:S(2)}) async-start(), calls=%async_computation.35 | async-start | bytes 2621440 | tf_op jit(solution)/shard_map/reduce_scatter | solution.py:368
  2783.5 122.3 %reduce-scatter.31.cloned.1.call-start = ((), (), s32[]{:S(2)}) async-start(), calls=%async_computation.34 | async-start | bytes 2621440 | tf_op jit(solution)/shard_map/reduce_scatter | solution.py:367
  2810.5 118.0 %reduce-scatter.53.cloned.1.call-start = ((), (), s32[]{:S(2)}) async-start(), calls=%async_computation.45 | async-start | bytes 163840
  2816.4 134.0 %reduce-scatter.49.cloned.1.call-start = ((), (), s32[]{:S(2)}) async-start(), calls=%async_computation.43 | async-start | bytes 81920
  2820.4 7.0 all-to-all-start.7
  2823.7 148.7 %reduce-scatter.47.cloned.1.call-start = ((), (), s32[]{:S(2)}) async-start(), calls=%async_computation.42 | async-start | bytes 81920
  2824.4 170.7 %reduce-scatter.51.cloned.1.call-start = ((), (), s32[]{:S(2)}) async-start(), calls=%async_computation.44 | async-start | bytes 163840
  2827.4 7.0 all-to-all-start.6
  2830.7 189.2 %reduce-scatter.43.cloned.1.call-start = ((), (), s32[]{:S(2)}) async-start(), calls=%async_computation.40 | async-start | bytes 655360
  2836.5 207.9 %reduce-scatter.45.cloned.1.call-start = ((), (), s32[]{:S(2)}) async-start(), calls=%async_computation.41 | async-start | bytes 655360
  2842.2 360.2 %all-reduce.52.cloned.1.call-start = ((), (), s32[]{:S(2)}) async-start(), calls=%async_computation.47 | async-start | bytes 8388608 | tf_op jit(solution)/shard_map/psum | solution.py:251
  2851.7 462.6 %all-reduce.50.cloned.1.call-start = ((), (), s32[]{:S(2)}) async-start(), calls=%async_computation.46 | async-start | bytes 8519680 | tf_op jit(solution)/shard_map/psum | solution.py:400
  (373 other events, 4934.6 us)
Sparse Core Ops, SparseCore 0:
  25.7 22.6 all-gather.15
  50.5 21.3 all-gather.11
  73.5 16.6 all-gather.13
  91.6 16.6 all-gather.17
  109.8 16.8 all-gather.19
  721.8 155.1 all-reduce.45
  878.6 18.0 all-gather.21
  898.2 19.0 all-gather.23
  918.8 19.0 all-gather.25
  952.0 154.9 all-reduce.47
  1109.5 34.9 reduce-scatter.36
  1146.9 36.0 reduce-scatter.38
  1185.6 35.9 reduce-scatter.40
  2754.0 23.7 reduce-scatter.28
  2780.3 24.8 reduce-scatter.26
  2807.5 31.1 reduce-scatter.34
  2841.1 31.1 reduce-scatter.32
  2874.7 31.1 reduce-scatter.30
  2908.9 19.6 reduce-scatter.52
  2930.8 19.5 reduce-scatter.48
  2952.8 19.5 reduce-scatter.46
  2975.4 19.6 reduce-scatter.50
  2998.2 21.6 reduce-scatter.42
  3022.8 21.6 reduce-scatter.44
  3047.4 154.9 all-reduce.51
  3205.3 108.9 all-reduce.49
where the time goes:
time: 3400 us; the launch traced here: 3330 us
  matrix products  997 us (29%)
  other arithmetic  874 us (26%)
  waiting for transfers between devices  793 us (23%)
  local copies, waits for them, and re-layouts  501 us (15%)
  blocking collectives  120 us (4%)
    dot_general x704, matrix products, matmul(): return jnp.dot(left, right, precision=lax.Precision.HIGHEST)  741 us
    another operation x160, other arithmetic, delta_block(): jax.scipy.linalg.solve_triangular(system, target, lower=True, unit_diagon...  381 us
    another operation x192, other arithmetic  193 us
    psum x1, waiting for transfers between devices, shards(): lax.psum(dot_plain(hidden, down_w).astype(jnp.bfloat16), 'tp')  157 us
    psum x1, waiting for transfers between devices, shards(): attended = lax.psum(dot_plain(gated_rows, out_w), 'tp')  148 us
    squeeze x160, local copies, waits for them, and re-layouts, delta_rule(): lax.scan(jax.checkpoint(delta_block), start_state, pieces)  146 us
    psum x1, waiting for transfers between devices, shards(): lax.psum(dot_back(grad_gate, gate_w) + dot_back(grad_up, up_w), 'tp')  144 us
    unnamed x32, waiting for transfers between devices  137 us
  transfers between devices with their start and end apart: 31, of which 20 were waited for; matrix products, arithmetic and copies ran while one was open for 69% of the time, Pallas kernels for 0%

commit v1 on v0

v1 whole, which is shorter than its diff:
```python
import functools
import jax
import jax.numpy as jnp
from jax import lax
from jax.experimental import pallas as pl
from jax.experimental.pallas import tpu as pltpu

F32 = jnp.float32
BF16 = jnp.bfloat16
CHUNK = 128
EPSILON = 1e-06
NN = (((1,), (0,)), ((), ()))
NT = (((1,), (1,)), ((), ()))
TN = (((0,), (0,)), ((), ()))


def mm(left, right, dims=NN):
    return lax.dot_general(
        left.astype(BF16), right.astype(BF16), dims, preferred_element_type=F32
    )


def iotas(size):
    rows = lax.broadcasted_iota(jnp.int32, (size, size), 0)
    cols = lax.broadcasted_iota(jnp.int32, (size, size), 1)
    return rows, cols


def to_row(column, eye):
    return jnp.sum(jnp.where(eye, column, 0.0), axis=0, keepdims=True)


def fades(decay, seg, before):
    size = decay.shape[0]
    rows, cols = iotas(size)
    eye = rows == cols
    decay_row = to_row(decay, eye)
    total_col = jnp.sum(jnp.where(cols <= rows, decay_row, 0.0), axis=1, keepdims=True)
    total_row = jnp.sum(jnp.where(rows <= cols, decay, 0.0), axis=0, keepdims=True)
    inside = (cols <= rows) & (seg == to_row(seg, eye))
    fading = jnp.where(inside, jnp.exp(jnp.minimum(total_col - total_row, 0.0)), 0.0)
    carried = before * jnp.exp(total_col)
    last_col = jnp.where(
        seg == seg[size - 1 :, :], jnp.exp(total_col[size - 1 :, :] - total_col), 0.0
    )
    return fading, carried, last_col


def inverses(lowers):
    size = lowers[0].shape[0]
    rows, cols = iotas(size)
    eye = jnp.where(rows == cols, 1.0, 0.0)
    totals = []
    pair = (rows // 2 == cols // 2) & (rows > cols)
    for lower in lowers:
        totals.append(eye - jnp.where(pair, lower, 0.0))
    half = 2
    while half < size:
        off = (rows // (2 * half) == cols // (2 * half)) & (rows // half > cols // half)
        lows = [t.astype(BF16) for t in totals]
        mids = [mm(jnp.where(off, lower, 0.0), t) for lower, t in zip(lowers, lows)]
        ends = [mm(t, mid) for t, mid in zip(lows, mids)]
        totals = [t - end for t, end in zip(totals, ends)]
        half *= 2
    return totals


def conv_rows(ext_ref, size, taps, masks):
    lines = [ext_ref[8 : 8 + size, :]]
    result = lines[0] * taps[0:1, :]
    for offset in (1, 2, 3):
        shifted = ext_ref[8 - offset : 8 - offset + size, :] * masks[offset - 1]
        result = result + shifted * taps[offset : offset + 1, :]
    return result


def unit_parts(silu, first, size):
    part = silu[:, first : first + size]
    return part, lax.rsqrt(jnp.sum(part * part, axis=1, keepdims=True) + EPSILON)


def prepare_kernel(
    sizes, raw_ref, halo_ref, aux_ref, taps_ref,
    unit_ref, val_ref, inv_ref, wu_ref, mix_ref, just_ref, state_ref, ext_ref,
):
    heads, dk, dv = sizes
    size = raw_ref.shape[0]

    @pl.when(pl.program_id(0) == 0)
    def _():
        ext_ref[0:8, :] = halo_ref[...].astype(F32)
        state_ref[...] = jnp.zeros_like(state_ref)

    @pl.when(pl.program_id(0) > 0)
    def _():
        ext_ref[0:8, :] = ext_ref[size : size + 8, :]

    ext_ref[8 : 8 + size, :] = raw_ref[...].astype(F32)
    aux = aux_ref[...]
    masks = [aux[:, 2 * heads + 2 + m : 2 * heads + 3 + m] for m in range(3)]
    conv = conv_rows(ext_ref, size, taps_ref[...], masks)
    silu = conv * jax.nn.sigmoid(conv)
    seg = aux[:, 2 * heads : 2 * heads + 1]
    before = aux[:, 2 * heads + 1 : 2 * heads + 2]
    rows, cols = iotas(size)
    val_ref[...] = silu[:, 2 * heads * dk :].astype(BF16)
    work = []
    for h in range(heads):
        beta = aux[:, h : h + 1]
        decay = aux[:, heads + h : heads + h + 1]
        q_part, q_norm = unit_parts(silu, h * dk, dk)
        k_part, k_norm = unit_parts(silu, (heads + h) * dk, dk)
        query = q_part * (q_norm * dk ** (-0.5))
        key = k_part * k_norm
        unit_ref[:, h * dk : (h + 1) * dk] = query.astype(BF16)
        unit_ref[:, (heads + h) * dk : (heads + h + 1) * dk] = key.astype(BF16)
        fading, carried, last_col = fades(decay, seg, before)
        both = mm(jnp.concatenate([key, query], axis=0), key, NT)
        just = jnp.where(rows > cols, fading * both[:size], 0.0)
        score = fading * both[size:]
        just_ref[:, h * size : (h + 1) * size] = just.astype(BF16)
        work.append((beta, query, key, carried, last_col, beta * just, score))
    totals = inverses([w[5] for w in work])
    for h, (beta, query, key, carried, last_col, lower, score) in enumerate(work):
        inv = totals[h].astype(BF16)
        inv_ref[:, h * size : (h + 1) * size] = inv
        value = silu[:, 2 * heads * dk + h * dv : 2 * heads * dk + (h + 1) * dv]
        right = jnp.concatenate([(beta * carried) * key, beta * value], axis=1)
        both = mm(inv, right).astype(BF16)
        wu_ref[:, h * (dk + dv) : (h + 1) * (dk + dv)] = both
        faded = jnp.transpose(key * last_col)
        left = jnp.concatenate([score, faded], axis=0).astype(BF16)
        prod = mm(left, both[:, :dk])
        q_eff = carried * query - prod[:size]
        top = jnp.concatenate([q_eff.astype(BF16), left[:size]], axis=1)
        low = jnp.concatenate([(-prod[size:]).astype(BF16), left[size:]], axis=1)
        mix_ref[0, h, 0:size, :] = top
        mix_ref[0, h, size : size + dk, :] = low
        state = state_ref[h]
        deep = jnp.concatenate([state.astype(BF16), both[:, dk:]], axis=0)
        state_ref[h] = carried[size - 1 :, :] * state + mm(low, deep)


def prepare(sizes, raw, halo, aux, taps):
    heads, dk, dv = sizes
    span, width = raw.shape
    blocks = span // CHUNK
    c = CHUNK
    rowed = lambda w: pl.BlockSpec((c, w), lambda i: (i, 0))
    fixed = lambda a: pl.BlockSpec(a.shape, lambda i: (0,) * a.ndim)
    return pl.pallas_call(
        functools.partial(prepare_kernel, sizes),
        grid=(blocks,),
        in_specs=[rowed(width), fixed(halo), rowed(aux.shape[1]), fixed(taps)],
        out_specs=[
            rowed(2 * heads * dk), rowed(heads * dv), rowed(heads * c),
            rowed(heads * (dk + dv)),
            pl.BlockSpec((1, heads, c + dk, c + dk), lambda i: (i, 0, 0, 0)),
            rowed(heads * c),
            pl.BlockSpec((heads, dk, dv), lambda i: (0, 0, 0)),
        ],
        out_shape=[
            jax.ShapeDtypeStruct((span, 2 * heads * dk), BF16),
            jax.ShapeDtypeStruct((span, heads * dv), BF16),
            jax.ShapeDtypeStruct((span, heads * c), BF16),
            jax.ShapeDtypeStruct((span, heads * (dk + dv)), BF16),
            jax.ShapeDtypeStruct((blocks, heads, c + dk, c + dk), BF16),
            jax.ShapeDtypeStruct((span, heads * c), BF16),
            jax.ShapeDtypeStruct((heads, dk, dv), F32),
        ],
        scratch_shapes=[pltpu.VMEM((c + 8, width), F32)],
        name="delta_prepare",
    )(raw, halo, aux, taps)


def apply_kernel(sizes, mix_ref, wu_ref, aux_ref, start_ref, out_ref, states_ref, state_ref):
    heads, dk, dv = sizes
    size = wu_ref.shape[0]

    @pl.when(pl.program_id(0) == 0)
    def _():
        state_ref[...] = start_ref[...]

    aux = aux_ref[...]
    for h in range(heads):
        decay = aux[:, heads + h : heads + h + 1]
        before = aux[size - 1 :, 2 * heads + 1 : 2 * heads + 2]
        through = before * jnp.exp(jnp.sum(decay, axis=0, keepdims=True))
        state = state_ref[h]
        low = state.astype(BF16)
        states_ref[0, h] = low
        first = h * (dk + dv) + dk
        deep = jnp.concatenate([low, wu_ref[:, first : first + dv]], axis=0)
        both = mm(mix_ref[0, h], deep)
        out_ref[:, h * dv : (h + 1) * dv] = both[:size].astype(BF16)
        state_ref[h] = through * state + both[size:]


def apply_states(sizes, mix, wu, aux, start):
    heads, dk, dv = sizes
    span = wu.shape[0]
    blocks = span // CHUNK
    c = CHUNK
    rowed = lambda w: pl.BlockSpec((c, w), lambda i: (i, 0))
    return pl.pallas_call(
        functools.partial(apply_kernel, sizes),
        grid=(blocks,),
        in_specs=[
            pl.BlockSpec((1, heads, c + dk, c + dk), lambda i: (i, 0, 0, 0)),
            rowed(wu.shape[1]), rowed(aux.shape[1]),
            pl.BlockSpec((heads, dk, dv), lambda i: (0, 0, 0)),
        ],
        out_specs=[
            rowed(heads * dv),
            pl.BlockSpec((1, heads, dk, dv), lambda i: (i, 0, 0, 0)),
            pl.BlockSpec((heads, dk, dv), lambda i: (0, 0, 0)),
        ],
        out_shape=[
            jax.ShapeDtypeStruct((span, heads * dv), BF16),
            jax.ShapeDtypeStruct((blocks, heads, dk, dv), BF16),
            jax.ShapeDtypeStruct((heads, dk, dv), F32),
        ],
        name="delta_apply",
    )(mix, wu, aux, start)


def back_chain_kernel(sizes, mix_ref, grad_ref, aux_ref, end_ref, state_ref):
    heads, dk, dv = sizes
    size = grad_ref.shape[0]

    @pl.when(pl.program_id(0) == 0)
    def _():
        state_ref[...] = end_ref[...]

    aux = aux_ref[...]
    for h in range(heads):
        decay = aux[:, heads + h : heads + h + 1]
        before = aux[size - 1 :, 2 * heads + 1 : 2 * heads + 2]
        through = before * jnp.exp(jnp.sum(decay, axis=0, keepdims=True))
        state = state_ref[h]
        deep = jnp.concatenate(
            [grad_ref[:, h * dv : (h + 1) * dv], state.astype(BF16)], axis=0
        )
        state_ref[h] = through * state + mm(mix_ref[0, h, :, 0:dk], deep, TN)


def back_chain(sizes, mix, grad, aux, end):
    heads, dk, dv = sizes
    span = grad.shape[0]
    blocks = span // CHUNK
    c = CHUNK
    last = blocks - 1
    rowed = lambda w: pl.BlockSpec((c, w), lambda i: (last - i, 0))
    return pl.pallas_call(
        functools.partial(back_chain_kernel, sizes),
        grid=(blocks,),
        in_specs=[
            pl.BlockSpec((1, heads, c + dk, c + dk), lambda i: (last - i, 0, 0, 0)),
            rowed(heads * dv), rowed(aux.shape[1]),
            pl.BlockSpec((heads, dk, dv), lambda i: (0, 0, 0)),
        ],
        out_specs=pl.BlockSpec((heads, dk, dv), lambda i: (0, 0, 0)),
        out_shape=jax.ShapeDtypeStruct((heads, dk, dv), F32),
        name="delta_back_chain",
    )(mix, grad, aux, end)


def back_kernel(
    sizes, raw_ref, prev_ref, halo_ref, aux_ref, taps_ref, unit_ref, val_ref, inv_ref, wu_ref,
    mix_ref, just_ref, states_ref, grad_ref, end_ref,
    draw_ref, tail_ref, head_ref, dtaps_ref, daux_ref,
    state_ref, ext_ref, next_ref, zext_ref, dsil_ref,
):
    heads, dk, dv = sizes
    size, width = raw_ref.shape
    step = pl.program_id(0)
    steps = pl.num_programs(0)

    @pl.when(step == 0)
    def _():
        state_ref[...] = end_ref[...]
        next_ref[...] = jnp.zeros_like(next_ref)
        dtaps_ref[...] = jnp.zeros_like(dtaps_ref)

    @pl.when(step == steps - 1)
    def _():
        ext_ref[0:8, :] = halo_ref[...].astype(F32)

    @pl.when(step < steps - 1)
    def _():
        ext_ref[0:8, :] = prev_ref[...].astype(F32)[8:, :]

    x = raw_ref[...].astype(F32)
    ext_ref[8 : 8 + size, :] = x
    aux = aux_ref[...]
    taps = taps_ref[...]
    masks = [aux[:, 2 * heads + 2 + m : 2 * heads + 3 + m] for m in range(3)]
    conv = conv_rows(ext_ref, size, taps, masks)
    sig = jax.nn.sigmoid(conv)
    silu = conv * sig
    seg = aux[:, 2 * heads : 2 * heads + 1]
    before = aux[:, 2 * heads + 1 : 2 * heads + 2]
    rows, cols = iotas(size)
    eye = rows == cols
    lanes = lax.broadcasted_iota(jnp.int32, (size, daux_ref.shape[1]), 1)
    is_last = lax.broadcasted_iota(jnp.int32, (size, 1), 0) == size - 1
    daux = jnp.zeros((size, daux_ref.shape[1]), F32)
    for h in range(heads):
        beta = aux[:, h : h + 1]
        decay = aux[:, heads + h : heads + h + 1]
        fading, carried, last_col = fades(decay, seg, before)
        query = unit_ref[:, h * dk : (h + 1) * dk]
        key = unit_ref[:, (heads + h) * dk : (heads + h + 1) * dk]
        value = val_ref[:, h * dv : (h + 1) * dv]
        inv = inv_ref[:, h * size : (h + 1) * size]
        weight = wu_ref[:, h * (dk + dv) : h * (dk + dv) + dk]
        upper = wu_ref[:, h * (dk + dv) + dk : (h + 1) * (dk + dv)]
        just = just_ref[:, h * size : (h + 1) * size].astype(F32)
        state_in = states_ref[0, h]
        dout = grad_ref[:, h * dv : (h + 1) * dv]
        dend = state_ref[h]
        dend_low = dend.astype(BF16)
        deep = jnp.concatenate([dout, dend_low], axis=0)
        both = mm(mix_ref[0, h], deep, TN)
        through = carried[size - 1 :, :]
        state_ref[h] = through * dend + both[:dk]
        dupd = both[dk:]
        update = (upper.astype(F32) - mm(weight, state_in)).astype(BF16)
        dres = mm(inv, dupd, TN)
        dres_low = dres.astype(BF16)
        left = jnp.concatenate([dout, dres_low], axis=0)
        right = jnp.concatenate([update, state_in], axis=0)
        quad = mm(left, right, NT)
        dscore = quad[:size, :size]
        dq_state = quad[:size, size:]
        dlower = jnp.where(rows > cols, -quad[size:, :size], 0.0)
        dk_state = quad[size:, size:]
        dfaded = mm(update, dend_low, NT)
        dqk = fading * dscore
        dkk = jnp.where(rows > cols, beta * fading, 0.0) * dlower
        query32 = query.astype(F32)
        key32 = key.astype(F32)
        score = mix_ref[0, h, 0:size, dk : dk + size].astype(F32)
        sym = dkk + jnp.transpose(dkk)
        pair = mm(jnp.concatenate([dqk, sym], axis=0), key)
        dquery = carried * dq_state + pair[:size]
        dkey = (
            last_col * dfaded
            + mm(dqk, query, TN)
            - (beta * carried) * dk_state
            + pair[size:]
        )
        kx = jnp.sum(key32 * dk_state, axis=1, keepdims=True)
        dcarried = jnp.sum(query32 * dq_state, axis=1, keepdims=True) - beta * kx
        dcarried = dcarried + jnp.where(
            is_last, jnp.sum(state_in.astype(F32) * dend), 0.0
        )
        dbeta = (
            jnp.sum(dlower * just, axis=1, keepdims=True)
            + jnp.sum(dres * value.astype(F32), axis=1, keepdims=True)
            - carried * kx
        )
        flow = dscore * score + dlower * (beta * just)
        kz = jnp.sum(key32 * dfaded, axis=1, keepdims=True) * last_col
        dtotal = jnp.sum(flow, axis=1, keepdims=True) + dcarried * carried - kz
        dtotal = dtotal + jnp.where(is_last, jnp.sum(kz, axis=0, keepdims=True), 0.0)
        dtotal_row = to_row(dtotal, eye) - jnp.sum(flow, axis=0, keepdims=True)
        ddecay = jnp.sum(jnp.where(cols >= rows, dtotal_row, 0.0), axis=1, keepdims=True)
        daux = daux + jnp.where(lanes == h, dbeta, 0.0)
        daux = daux + jnp.where(lanes == heads + h, ddecay, 0.0)
        dsil_ref[:, 2 * heads * dk + h * dv : 2 * heads * dk + (h + 1) * dv] = beta * dres
        for first, grad, scale in ((h, dquery, dk ** (-0.5)), (heads + h, dkey, 1.0)):
            part, norm = unit_parts(silu, first * dk, dk)
            unit = part * norm
            grad = grad * scale
            inner = jnp.sum(unit * grad, axis=1, keepdims=True)
            dsil_ref[:, first * dk : (first + 1) * dk] = norm * (grad - unit * inner)
    daux_ref[...] = daux
    dconv = dsil_ref[...] * (sig * (1.0 + conv * (1.0 - sig)))
    draw = dconv * taps[0:1, :]
    dtaps_ref[0:1, :] += jnp.sum(dconv * x, axis=0, keepdims=True)
    halo = halo_ref[...].astype(F32)
    head = jnp.zeros((8, width), F32)
    for m in (1, 2, 3):
        moved = dconv * masks[m - 1]
        zext_ref[8 : 8 + size, :] = moved
        zext_ref[8 + size :, :] = next_ref[m - 1]
        next_ref[m - 1] = moved[0:8, :]
        shifted = zext_ref[8 + m : 8 + m + size, :]
        draw = draw + shifted * taps[m : m + 1, :]
        dtaps_ref[m : m + 1, :] += jnp.sum(shifted * x, axis=0, keepdims=True)

        @pl.when(step == steps - 1)
        def _():
            zext_ref[0:8, :] = jnp.zeros((8, width), F32)
            edge = zext_ref[m : m + 8, :]
            dtaps_ref[m : m + 1, :] += jnp.sum(edge * halo, axis=0, keepdims=True)
            grown = edge * taps[m : m + 1, :]
            if m == 1:
                head_ref[...] = grown
            else:
                head_ref[...] += grown

    draw_ref[...] = draw.astype(BF16)

    @pl.when(step == 0)
    def _():
        tail_ref[...] = draw[size - 8 :, :]


def back_states(sizes, raw, halo, aux, taps, unit, val, inv, wu, mix, just, states, grad, end):
    heads, dk, dv = sizes
    span, width = raw.shape
    blocks = span // CHUNK
    c = CHUNK
    last = blocks - 1
    rowed = lambda w: pl.BlockSpec((c, w), lambda i: (last - i, 0))
    fixed = lambda shape: pl.BlockSpec(shape, lambda i: (0,) * len(shape))
    per16 = c // 16
    prev = pl.BlockSpec((16, width), lambda i: (jnp.maximum((last - i) * per16 - 1, 0), 0))
    return pl.pallas_call(
        functools.partial(back_kernel, sizes),
        grid=(blocks,),
        in_specs=[
            rowed(width), prev, fixed(halo.shape), rowed(aux.shape[1]), fixed(taps.shape),
            rowed(unit.shape[1]), rowed(val.shape[1]), rowed(inv.shape[1]), rowed(wu.shape[1]),
            pl.BlockSpec((1, heads, c + dk, c + dk), lambda i: (last - i, 0, 0, 0)),
            rowed(just.shape[1]),
            pl.BlockSpec((1, heads, dk, dv), lambda i: (last - i, 0, 0, 0)),
            rowed(heads * dv), fixed(end.shape),
        ],
        out_specs=[
            rowed(width), fixed((8, width)), fixed((8, width)), fixed((8, width)), rowed(8),
        ],
        out_shape=[
            jax.ShapeDtypeStruct((span, width), BF16),
            jax.ShapeDtypeStruct((8, width), F32),
            jax.ShapeDtypeStruct((8, width), F32),
            jax.ShapeDtypeStruct((8, width), F32),
            jax.ShapeDtypeStruct((span, 8), F32),
        ],
        scratch_shapes=[
            pltpu.VMEM((heads, dk, dv), F32),
            pltpu.VMEM((c + 8, width), F32),
            pltpu.VMEM((3, 8, width), F32),
            pltpu.VMEM((c + 16, width), F32),
            pltpu.VMEM((c, width), F32),
        ],
        name="delta_back",
    )(raw, raw, halo, aux, taps, unit, val, inv, wu, mix, just, states, grad, end)


from jax.sharding import PartitionSpec as P


def dot_plain(left, right):
    return jnp.dot(left, right, preferred_element_type=F32)


def dot_back(left, right):
    return lax.dot_general(left, right, NT, preferred_element_type=F32)


def dot_outer(left, right):
    return lax.dot_general(left, right, TN, preferred_element_type=F32)


def rms_norm(vector, scale_gain):
    return (
        vector * lax.rsqrt(jnp.mean(vector * vector, axis=-1, keepdims=True) + EPSILON) * scale_gain
    )


def gated_norm(mixed_in, gate_in, gain_in, live_rows):
    head_count = gain_in.shape[0]
    per_head = mixed_in.reshape(mixed_in.shape[0], head_count, -1)
    gated_rows = rms_norm(per_head, gain_in) * jax.nn.silu(gate_in).reshape(per_head.shape)
    return (gated_rows * live_rows[:, None, None]).reshape(mixed_in.shape)


def gate_rates(beta_lin, decay_lin, bias_in):
    return (jax.nn.sigmoid(beta_lin), -jax.nn.softplus(decay_lin + bias_in))


def row_facts(segment_ids, first, span):
    def at(offset):
        moved = segment_ids
        if offset:
            moved = jnp.concatenate(
                [jnp.full((offset,), -2, jnp.int32), segment_ids[:-offset]], axis=0
            )
        return lax.dynamic_slice_in_dim(moved, first, span)

    here = at(0)
    before = jnp.repeat(at(1).reshape(-1, CHUNK)[:, 0], CHUNK)
    flags = [here == before] + [here == at(m) for m in (1, 2, 3)]
    return here, [here.astype(F32)] + [f.astype(F32) for f in flags]


def scatter_sum(parts, axis):
    low = parts.astype(BF16)
    out = lax.psum_scatter(low, "shard", scatter_dimension=axis, tiled=True)
    return lax.psum(out, "ctx").astype(F32)


def shards(
    tokens, segment_ids, cotangent, norm_gain, w_query, w_key, w_value, w_outgate, w_beta, w_decay,
    decay_bias, conv_query, conv_key, conv_value, out_gain, w_out, mlp_gain, w_gate, w_up, w_down,
):
    ctx_size = lax.axis_size("ctx")
    ctx_rank = lax.axis_index("ctx")
    shard_size = lax.axis_size("shard")
    rows_here, model = tokens.shape
    heads = decay_bias.shape[0]
    dk = conv_query.shape[2] * shard_size
    dv = conv_value.shape[2] * shard_size
    sizes = (heads, dk, dv)
    gather = lambda v, axis: lax.all_gather(v, "shard", axis=axis, tiled=True)
    mixer_w = gather(jnp.concatenate([w_query, w_key, w_value, w_outgate], axis=1), 0)
    mlp_w = gather(jnp.concatenate([w_gate, w_up], axis=1), 0)
    out_w = gather(w_out, 1)
    down_w = gather(w_down, 1)
    tiny = [norm_gain, mlp_gain, w_beta, w_decay, conv_query, conv_key, conv_value, out_gain]
    flat = jnp.concatenate([v.reshape(-1) for v in tiny])
    flat = lax.all_gather(flat, "shard", axis=0)
    cuts, at = [], 0
    for v in tiny:
        cuts.append(flat[:, at : at + v.size].reshape((shard_size,) + v.shape))
        at += v.size
    gain_one = cuts[0].reshape(-1).astype(F32)
    gain_two = cuts[1].reshape(-1).astype(F32)
    small_w = jnp.concatenate([cuts[2], cuts[3]], axis=2).reshape(model, 2 * heads)
    taps = [jnp.moveaxis(c, 0, 2).reshape(c.shape[1], -1) for c in cuts[4:7]]
    taps = jnp.concatenate(taps, axis=1).astype(F32)
    head_gain = jnp.moveaxis(cuts[7], 0, 1).reshape(heads, dv).astype(F32)
    conv_width = taps.shape[1]

    here, facts = row_facts(segment_ids, ctx_rank * rows_here, rows_here)
    live_rows = (here >= 0).astype(F32)
    inputs32 = tokens.astype(F32)
    normed32, norm_one_back = jax.vjp(rms_norm, inputs32, gain_one)
    normed = normed32.astype(BF16)
    raw = dot_plain(normed, mixer_w[:, :conv_width]).astype(BF16)
    gate_raw = dot_plain(normed, mixer_w[:, conv_width:])
    small_lin = dot_plain(normed, small_w)
    (beta_rows, decays), rates_back = jax.vjp(
        gate_rates, small_lin[:, :heads], small_lin[:, heads:], decay_bias.astype(F32)
    )
    low = lambda v: v.astype(BF16).astype(F32)
    columns = [low(beta_rows)[:, h] for h in range(heads)]
    columns += [low(decays)[:, h] for h in range(heads)] + facts
    columns += [jnp.zeros((rows_here,), F32)] * (16 - len(columns))
    aux = jnp.stack(columns, axis=1)
    ahead = [(i, i + 1) for i in range(ctx_size - 1)]
    behind = [(i + 1, i) for i in range(ctx_size - 1)]
    halo = lax.ppermute(raw[rows_here - 8 :], "ctx", ahead)
    unit, val, inv, wu, mix, just, total = prepare(sizes, raw, halo, aux, taps)
    start = lax.ppermute(total, "ctx", ahead)
    for _ in range(ctx_size - 2):
        start = lax.ppermute(apply_states(sizes, mix, wu, aux, start)[2], "ctx", ahead)
    mixed, states, _ = apply_states(sizes, mix, wu, aux, start)

    gated32, gated_back = jax.vjp(
        lambda mixed_in, gate_in, gain_in: gated_norm(mixed_in, gate_in, gain_in, live_rows),
        mixed.astype(F32), gate_raw, head_gain,
    )
    gated_rows = gated32.astype(BF16)
    attended = lax.psum(dot_plain(gated_rows, out_w).astype(BF16), "tp").astype(F32)
    hidden_in = inputs32 + attended
    normed_two32, norm_two_back = jax.vjp(rms_norm, hidden_in, gain_two)
    normed_two = normed_two32.astype(BF16)
    both_two = dot_plain(normed_two, mlp_w)
    units = w_gate.shape[1]
    gate_two, up_two = both_two[:, :units], both_two[:, units:]
    sigmoid_two = jax.nn.sigmoid(gate_two)
    activated = gate_two * sigmoid_two
    hidden = (activated * up_two).astype(BF16)
    mlp_out = lax.psum(dot_plain(hidden, down_w).astype(BF16), "tp").astype(F32)
    result = (hidden_in + mlp_out).astype(BF16)
    grad_hidden = dot_back(cotangent, down_w)
    gate_slope = sigmoid_two * (1.0 + gate_two * (1.0 - sigmoid_two))
    grad_gate = (grad_hidden * up_two * gate_slope).astype(BF16)
    grad_up = (grad_hidden * activated).astype(BF16)
    grad_both = jnp.concatenate([grad_gate, grad_up], axis=1)
    part_mlp = scatter_sum(dot_outer(normed_two, grad_both), 0)
    part_down = scatter_sum(dot_outer(hidden, cotangent), 1)
    grad_normed_two = lax.psum(dot_back(grad_both, mlp_w).astype(BF16), "tp").astype(F32)
    grad_hidden_in, grad_gain_two = norm_two_back(grad_normed_two)
    grad_hidden_in = grad_hidden_in + cotangent.astype(F32)
    grad_branch = grad_hidden_in.astype(BF16)
    part_out = scatter_sum(dot_outer(gated_rows, grad_branch), 1)
    grad_gated = dot_back(grad_branch, out_w)
    grad_mixed, grad_gate_raw, grad_head_gain = gated_back(grad_gated)
    grad_mixed = grad_mixed.astype(BF16)
    zero = jnp.zeros((heads, dk, dv), F32)
    end = lax.ppermute(back_chain(sizes, mix, grad_mixed, aux, zero), "ctx", behind)
    for _ in range(ctx_size - 2):
        end = lax.ppermute(back_chain(sizes, mix, grad_mixed, aux, end), "ctx", behind)
    draw, tail, head, dtaps, daux = back_states(
        sizes, raw, halo, aux, taps, unit, val, inv, wu, mix, just, states, grad_mixed, end
    )
    tail = (tail + lax.ppermute(head, "ctx", behind)).astype(BF16)
    draw = lax.dynamic_update_slice(draw, tail, (rows_here - 8, 0))
    grad_gate_low = grad_gate_raw.astype(BF16)
    grad_beta_lin, grad_decay_lin, grad_bias = rates_back(
        (daux[:, :heads], daux[:, heads : 2 * heads])
    )
    grad_small = jnp.concatenate([grad_beta_lin, grad_decay_lin], axis=1).astype(BF16)
    grad_mix = jnp.concatenate([draw, grad_gate_low], axis=1)
    grad_mixer_w = dot_outer(normed, grad_mix)
    grad_small_w = dot_outer(normed, grad_small)
    grad_normed_part = dot_back(grad_mix, mixer_w) + dot_back(grad_small, small_w)
    grad_normed = lax.psum(grad_normed_part.astype(BF16), "tp").astype(F32)
    grad_inputs, grad_gain_one = norm_one_back(grad_normed)
    input_grad = grad_inputs + grad_hidden_in
    part_mixer = scatter_sum(grad_mixer_w, 0)
    split = lambda v: v.reshape(shard_size, -1)
    taps_parts = []
    first = 0
    for width in (heads * dk, heads * dk, heads * dv):
        part = dtaps[:4, first : first + width].reshape(4, heads, shard_size, -1)
        taps_parts.append(jnp.moveaxis(part, 2, 0))
        first += width
    tiny_grads = [
        split(grad_gain_one), split(grad_gain_two), split(grad_small_w),
        split(jnp.broadcast_to(grad_bias[None], (shard_size, heads))),
        *[split(p) for p in taps_parts],
        split(jnp.moveaxis(grad_head_gain.reshape(heads, shard_size, -1), 1, 0)),
    ]
    shapes = [
        norm_gain.shape, mlp_gain.shape, (w_beta.shape[0], 2 * heads), decay_bias.shape,
        conv_query.shape, conv_key.shape, conv_value.shape, out_gain.shape,
    ]
    packed = jnp.concatenate(tiny_grads, axis=1)
    packed = lax.psum(packed, ("shard", "ctx"))
    mine = lax.dynamic_slice_in_dim(packed, lax.axis_index("shard"), 1, 0)[0]
    small, at = [], 0
    for shape in shapes:
        count = 1
        for n in shape:
            count *= n
        small.append(mine[at : at + count].reshape(shape))
        at += count
    qw, vw = heads * dk, heads * dv
    return (
        result,
        input_grad,
        small[0],
        part_mixer[:, :qw],
        part_mixer[:, qw : 2 * qw],
        part_mixer[:, 2 * qw : 2 * qw + vw],
        part_mixer[:, 2 * qw + vw :],
        small[2][:, :heads],
        small[2][:, heads:],
        small[3],
        small[4],
        small[5],
        small[6],
        small[7],
        part_out,
        small[1],
        part_mlp[:, :units],
        part_mlp[:, units:],
        part_down,
    )


def solution(mesh):
    rows = P(("shard", "ctx"), None)
    cols = P("shard", "tp")
    taps = P(None, "tp", "shard")
    turned = P("tp", "shard")
    in_specs = (
        rows, P("shard"), rows, P("shard"), cols, cols, cols, cols, cols, cols, P("tp"),
        taps, taps, taps, turned, turned, P("shard"), cols, cols, turned,
    )
    out_specs = (
        rows, rows, P("shard"), cols, cols, cols, cols, cols, cols, P("tp"),
        taps, taps, taps, turned, turned, P("shard"), cols, cols, turned,
    )
    return jax.shard_map(shards, mesh=mesh, in_specs=in_specs, out_specs=out_specs, check_vma=False)
```

time: 3400 us -> 767 us (0.23); the launches traced: 3330 us -> 759 us
  matrix products: 997 us -> 78.4 us
  other arithmetic: 874 us -> 50.3 us
  local copies, waits for them, and re-layouts: 501 us -> 61 us
  waiting for transfers between devices: 793 us -> 433 us
  blocking collectives: 120 us -> 33.4 us
  Pallas kernels: 0 us -> 70 us
    dot_general x763 -> x16, matrix products: 869 us -> 78.4 us  [the longest x6 27.2 us: dot_plain(): return jnp.dot(left, right, preferred_element_type=F32)]
    another operation x384 -> x2, other arithmetic: 602 us -> 0.11 us  [the longest x1 0.09 us: shards(): aux = jnp.stack(columns, axis=1)]
    psum x4, waiting for transfers between devices: 528 us -> 344 us  [the longest x1 157 us: shards(): mlp_out = lax.psum(dot_plain(hidden, down_w).astype(BF16), 'tp').astype(F32)]
    squeeze x161 -> x0, local copies, waits for them, and re-layouts: 147 us -> none  [the longest x160 146 us: delta_rule(): lax.scan(jax.checkpoint(delta_block), start_state, pieces)]
    unnamed x32 -> x12, waiting for transfers between devices: 137 us -> 1.39 us
    another operation x128 -> x0, matrix products: 128 us -> none  [delta_block(): jax.scipy.linalg.solve_triangular(system, target, lower=True, unit_diagon...]
    dynamic_update_slice x66 -> x0, local copies, waits for them, and re-layouts: 80.9 us -> none  [the longest x64 80.8 us: delta_rule(): lax.scan(jax.checkpoint(delta_block), start_state, pieces)]
    dynamic_slice x64 -> x0, local copies, waits for them, and re-layouts: 78.4 us -> none  [delta_rule(): lax.scan(jax.checkpoint(delta_block), start_state, pieces)]
  transfers between devices with their start and end apart: 31 -> 16, of which waited for: 20 -> 10; matrix products, arithmetic and copies ran while one was open for 69% -> 20% of each run, Pallas kernels for 0% -> 9%
where the time goes in v1:
time: 767 us; the launch traced here: 759 us
  waiting for transfers between devices  433 us (56%)
  matrix products  78.4 us (10%)
  Pallas kernels  70 us (9%)
  local copies, waits for them, and re-layouts  61 us (8%)
  other arithmetic  50.3 us (7%)
  blocking collectives  33.4 us (4%)
  starting transfers between devices  18.6 us (2%)
  between operations  15.1 us (2%)
    psum x1, waiting for transfers between devices, shards(): mlp_out = lax.psum(dot_plain(hidden, down_w).astype(BF16), 'tp').astype(F32)  157 us
    psum x1, waiting for transfers between devices, shards(): lax.psum(dot_plain(gated_rows, out_w).astype(BF16), 'tp').astype(F32)  82.7 us
    psum x1, waiting for transfers between devices, shards(): lax.psum(dot_back(grad_both, mlp_w).astype(BF16), 'tp').astype(F32)  81.1 us
    all_gather x4, waiting for transfers between devices, shards(): gather = lambda v, axis: lax.all_gather(v, 'shard', axis=axis, tiled=True)  54.5 us
    pallas_call x1, Pallas kernels, back_states(): pl.pallas_call(functools.partial(back_kernel, sizes), grid=(blocks,), in_...  32 us
    psum x1, blocking collectives, shards(): packed = lax.psum(packed, ('shard', 'ctx'))  27.2 us
    dot_general x6, matrix products, dot_plain(): return jnp.dot(left, right, preferred_element_type=F32)  27.2 us
    dot_general x5, matrix products, dot_back(): return lax.dot_general(left, right, NT, preferred_element_type=F32)  26 us
  transfers between devices with their start and end apart: 16, of which 10 were waited for; matrix products, arithmetic and copies ran while one was open for 20% of the time, Pallas kernels for 9%

profile of v1, /device:TPU:0, one launch (start us, length us, event | category | flops | bytes accessed | tf_op | source)
XLA Modules:
  0.0 759.5 jit_solution(2950109026487284267)
XLA Ops:
  13.0 6.2 all-gather.1
  25.1 16.4 %all-gather.7.cloned.1.call-done = bf16[1024,1536]{1,0:T(8,128)(2,1)} async-done(((bf16[256,1536]{1,0:T(8,128)(2,1)}), bf16[1024,1536]{1,0:T(8,128)(2,1)}) %all-gather.7.cloned.1.call-update) | async-done | bytes 3145744 | tf_op jit(solution)/shard_map/all_gather | solution.py:518
  57.1 4.7 stack.44.aux_ref
  62.4 24.7 %delta_prepare.1 = (bf16[1024,512]{1,0:T(8,128)(2,1)}, bf16[1024,512]{1,0:T(8,128)(2,1)}, bf16[1024,256]{1,0:T(8,128)(2,1)}, bf16[1024,768]{1,0:T(8,128)(2,1)}, ...) custom-call(bf16[1024,1024]{1,0:T(8,128)(2,1)} %copy-done.1, ...), custom_call_target="tpu_custom_call" | custom-call | tf_op jit(solution)/shard_map/delta_prepare/pallas_call | solution.py:151
  87.1 11.3 %collective-permute-start.1 = (f32[2,128,256]{2,1,0:T(8,128)}, f32[2,128,256]{2,1,0:T(8,128)S(1)}, u32[]{:S(2)}, u32[]{:S(2)}) collective-permute-start(f32[2,128,256]{2,1,0:T(8,128)} %get-tuple-element.35), channel_id=1, source_target_pairs={{0,4},{1,5},{2,6},{3,7},{8,12},{9,13},{10,14},{11,15},{16,20},{17,... | collective-permute-start | bytes 786440 | tf_op jit(solution)/shard_map/ppermute | solution.py:558
  99.3 6.8 delta_apply.1
  115.4 4.9 fusion.19
  127.1 82.7 %all-reduce.9.cloned.1.call-done = bf16[1024,1024]{1,0:T(8,128)(2,1)} async-done(((bf16[1024,1024]{1,0:T(8,128)(2,1)}), bf16[1024,1024]{1,0:T(8,128)(2,1)}) %all-reduce.9.cloned.1.call-update) | async-done | bytes 2097168 | tf_op jit(solution)/shard_map/psum | solution.py:568
  212.2 26.1 %all-gather.11.cloned.1.call-done = bf16[1024,1408]{0,1:T(8,128)(2,1)} async-done(((bf16[256,1408]{0,1:T(8,128)(2,1)}), bf16[1024,1408]{0,1:T(8,128)(2,1)}) %all-gather.11.cloned.1.call-update) | async-done | bytes 2883600 | tf_op jit(solution)/shard_map/all_gather | solution.py:518
  238.3 8.4 %fusion.57 = f32[1024,1408]{1,0:T(8,128)} fusion(bf16[1024,1408]{0,1:T(8,128)(2,1)} %all-gather.11.cloned.1.call-done, bf16[1024,1024]{1,0:T(8,128)(2,1)} %all-reduce.9.cloned.1.call-done, bf16[1024,1024]{1,0:T(8,128)(2,1)S(1)} %copy-done, f32[1024]{0:T(1024)S(1)} %bitcast.69, f32[1024]{0:T(1024)S(1)} %fusion.45), kind=kOutput, calls=%fused_computation.132 | convolution fusion | flops 2959081472 | bytes 12853248 | tf_op jit(solution)/shard_map/dot_general | solution.py:457
  246.7 12.1 %all-gather.13.cloned.1.call-done = bf16[704,1024]{1,0:T(8,128)(2,1)} async-done(((bf16[704,256]{1,0:T(8,128)(2,1)}), bf16[704,1024]{1,0:T(8,128)(2,1)}) %all-gather.13.cloned.1.call-update) | async-done | bytes 1441808 | tf_op jit(solution)/shard_map/all_gather | solution.py:518
  258.8 7.7 %multiply_convert_fusion.2 = (bf16[1024,704]{1,0:T(8,128)(2,1)S(1)}, bf16[1024,704]{1,0:T(8,128)(2,1)S(1)}, bf16[1024,704]{1,0:T(8,128)(2,1)}) fusion(f32[1024,1408]{1,0:T(8,128)} %fusion.57, bf16[1024,1024]{1,0:T(8,128)(2,1)} %param.22, bf16[704,1024]{1,0:T(8,128)(2,1)} %all-gather.13.cloned.1.call-done), kind=kOutput, calls=%fused_computation.33 | convolution fusion | flops 1487208448 | bytes 13631488 | tf_op jit(solution)/shard_map/dot_general | solution.py:461
  268.1 4.7 convolution_convert_fusion.2
  272.9 4.9 convolution_convert_fusion.5
  278.1 81.1 %all-reduce.11.cloned.1.call-done = bf16[1024,1024]{1,0:T(8,128)(2,1)} async-done(((bf16[1024,1024]{1,0:T(8,128)(2,1)}), bf16[1024,1024]{1,0:T(8,128)(2,1)}) %all-reduce.11.cloned.1.call-update) | async-done | bytes 2097168 | tf_op jit(solution)/shard_map/psum | solution.py:587
  363.3 4.2 convolution_convert_fusion.6
  367.6 8.2 %convolution_convert_fusion = bf16[1024,1408]{1,0:T(8,128)(2,1)} fusion(bf16[1024,704]{1,0:T(8,128)(2,1)} %copy-done.35, bf16[1024,704]{1,0:T(8,128)(2,1)} %copy-done.34, bf16[1024,1024]{1,0:T(8,128)(2,1)} %all-reduce.9.cloned.1.call-done, bf16[1024,1024]{1,0:T(8,128)(2,1)S(1)} %copy-done, f32[1024]{0:T(1024)S(1)} %bitcast.72, f32[1024]{0:T(1024)S(1)} %fusion.45), kind=kOutput, calls=%fused_computation.27 | convolution fusion | flops 2966290432 | bytes 9969664 | tf_op jit(solution)/shard_map/dot_general | solution.py:465
  380.1 6.5 fusion.27
  393.6 16.0 %multiply_reduce_fusion.2 = f32[1024,2]{1,0:T(8,128)S(1)} fusion(f32[1024,2,256]{2,1,0:T(2,128)} %reshape.285, f32[1024,2,256]{2,1,0:T(2,128)} %reshape.287, f32[1024,2,256]{2,1,0:T(2,128)} %copy.250, f32[1024]{0:T(1024)S(1)} %get-tuple-element.231, f32[2,256]{1,0:T(2,128)S(1)} %reshape.311), kind=kLoop, calls=%fused_computation.45 | loop fusion | flops 2619392 | bytes 6305792 | tf_op jit(solution)/shard_map/transpose(jvp())/reduce_sum | solution.py:470
  413.6 4.6 fusion.16
  418.9 6.4 delta_back_chain.1
  426.6 8.6 %collective-permute-done.2.end_ref = f32[2,128,256]{2,1,0:T(8,128)S(1)} collective-permute-done((f32[2,128,256]{2,1,0:T(8,128)}, f32[2,128,256]{2,1,0:T(8,128)S(1)}, u32[]{:S(2)}, u32[]{:S(2)}) %collective-permute-start.2) | collective-permute-done | bytes 262176 | tf_op jit(solution)/shard_map/ppermute | solution.py:596
  435.9 32.0 %delta_back.1 = (bf16[1024,1024]{1,0:T(8,128)(2,1)}, f32[8,1024]{1,0:T(8,128)}, f32[8,1024]{1,0:T(8,128)}, f32[8,1024]{1,0:T(8,128)}, f32[1024,8]{1,0:T(8,128)}) custom-call(bf16[1024,1024]{1,0:T(8,128)(2,1)} %copy-done.1, bf16[1024,1024]{1,0:T(8,128)(2,1)} %copy-done.1, bf16[8,1024]{1,0:T(8,128)(2,1)} %copy-done.21, f32[1024,16]{1,0:T(8,128)} %stack.44.aux_ref, ...), custom_call_target="tpu_custom_call" | custom-call | tf_op jit(solution)/shard_map/delta_back/pallas_call | solution.py:421
  469.5 4.7 collective-permute-done.3
  475.5 7.0 convolution_convert_fusion.1
  484.1 5.0 convolution_convert_fusion.4
  492.5 6.3 add_convert_fusion
  500.1 18.9 %reduce-scatter.5.cloned.1.call-done = bf16[256,1536]{1,0:T(8,128)(2,1)} async-done(((bf16[1024,1536]{1,0:T(8,128)(2,1)}), bf16[256,1536]{1,0:T(8,128)(2,1)}) %reduce-scatter.5.cloned.1.call-update) | async-done | bytes 786448 | tf_op jit(solution)/shard_map/reduce_scatter | solution.py:502
  519.9 157.1 %all-reduce.13.cloned.1.call-done = (bf16[1024,1024]{1,0:T(8,128)(2,1)}, bf16[1024,1024]{1,0:T(8,128)(2,1)}) async-done(((bf16[1024,1024]{1,0:T(8,128)(2,1)}, bf16[1024,1024]{1,0:T(8,128)(2,1)}), (bf16[1024,1024]{1,0:T(8,128)(2,1)}, bf16[1024,1024]{1,0:T(8,128)(2,1)})) %all-reduce.13.cloned.1.call-update) | async-done | bytes 4194320 | tf_op jit(solution)/shard_map/psum | solution.py:578
  680.4 27.2 %psum.67 = f32[4,2690]{1,0:T(4,128)S(1)} all-reduce(f32[4,2690]{1,0:T(4,128)S(1)} %concatenate.56), channel_id=1, replica_groups=mesh['shard'=4,'ctx'=2,'tp'=4] {'shard','ctx'}, use_global_device_ids=true, to_apply=%region_14.15 | all-reduce | flops 10760 | bytes 86080 | tf_op jit(solution)/shard_map/psum | solution.py:635
  713.4 7.2 fusion.9
  720.6 23.5 %all-reduce.15.cloned.1.call-done = (bf16[256,1536]{1,0:T(8,128)(2,1)}, bf16[256,1408]{1,0:T(8,128)(2,1)}, bf16[512,256]{1,0:T(8,128)(2,1)}, bf16[704,256]{1,0:T(8,128)(2,1)}) async-done(((bf16[256,1536]{1,0:T(8,128)(2,1)}, bf16[256,1408]{1,0:T(8,128)(2,1)}, bf16[512,256]{1,0:T(8,128)(2,1)}, bf16[704,256]{1,0:T(8,128)(2,1)}), (bf16[256,1536]{1,0:T(8,128)(2,1)}, bf16[256,1408]{1,0:T(8,128)(2,1)}, ...) | async-done | bytes 2129936 | tf_op jit(solution)/shard_map/psum | solution.py:503
  (239 shorter events, 98.1 us)
Async XLA Ops:
  7.2 3.5 copy-start.26
  7.2 3.8 copy-start.27
  7.3 4.1 copy-start.28
  7.3 4.3 copy-start.29
  7.3 12.0 %copy-start.33 = (bf16[2]{0:T(256)(128)(2,1)S(1)}, bf16[2]{0:T(256)(128)(2,1)}, u32[]{:S(2)}) copy-start(bf16[2]{0:T(256)(128)(2,1)} %param.30) | copy-start | bytes 16
  7.3 12.0 %copy-start = (bf16[1024,1024]{1,0:T(8,128)(2,1)S(1)}, bf16[1024,1024]{1,0:T(8,128)(2,1)}, u32[]{:S(2)}) copy-start(bf16[1024,1024]{1,0:T(8,128)(2,1)} %param.20) | copy-start | bytes 6291460
  7.3 34.2 %all-gather.7.cloned.1.call-start = ((), (), s32[]{:S(2)}) async-start(), calls=%async_computation.4 | async-start | bytes 3932160 | tf_op jit(solution)/shard_map/all_gather | solution.py:518
  9.5 10.3 %copy-start.20 = (s32[2048]{0:T(1024)S(1)}, s32[2048]{0:T(1024)}, u32[]{:S(2)}) copy-start(s32[2048]{0:T(1024)} %param.21) | copy-start | bytes 24580
  9.6 110.8 %all-gather.9.cloned.1.call-start = ((), (), s32[]{:S(2)}) async-start(), calls=%async_computation.5 | async-start | bytes 1310720 | tf_op jit(solution)/shard_map/all_gather | solution.py:518
  10.3 199.5 %all-reduce.9.cloned.1.call-start = ((), (), s32[]{:S(2)}) async-start(), calls=%async_computation.6 | async-start | bytes 4194304 | tf_op jit(solution)/shard_map/psum | solution.py:568
  46.8 14.9 %collective-permute-start = (bf16[8,1024]{1,0:T(8,128)(2,1)S(1)}, bf16[8,1024]{1,0:T(8,128)(2,1)S(1)}, u32[]{:S(2)}, u32[]{:S(2)}) collective-permute-start(bf16[8,1024]{1,0:T(8,128)(2,1)S(1)} %slice.186), channel_id=1, source_target_pairs={{0,4},{1,5},{2,6},{3,7},{8,12},{9,13},{10,14},{11,15},{16,20},{17,... | collective-permute-start | bytes 49160 | tf_op jit(solution)/shard_map/ppermute | solution.py:556
  87.1 11.5 %collective-permute-start.1 = (f32[2,128,256]{2,1,0:T(8,128)}, f32[2,128,256]{2,1,0:T(8,128)S(1)}, u32[]{:S(2)}, u32[]{:S(2)}) collective-permute-start(f32[2,128,256]{2,1,0:T(8,128)} %get-tuple-element.35), channel_id=1, source_target_pairs={{0,4},{1,5},{2,6},{3,7},{8,12},{9,13},{10,14},{11,15},{16,20},{17,... | collective-permute-start | bytes 786440 | tf_op jit(solution)/shard_map/ppermute | solution.py:558
  124.5 113.8 %all-gather.11.cloned.1.call-start = ((), (), s32[]{:S(2)}) async-start(), calls=%async_computation.7 | async-start | bytes 3604480 | tf_op jit(solution)/shard_map/all_gather | solution.py:518
  126.5 132.3 %all-gather.13.cloned.1.call-start = ((), (), s32[]{:S(2)}) async-start(), calls=%async_computation.8 | async-start | bytes 1802240 | tf_op jit(solution)/shard_map/all_gather | solution.py:518
  127.1 232.0 %all-reduce.11.cloned.1.call-start = ((), (), s32[]{:S(2)}) async-start(), calls=%async_computation.9 | async-start | bytes 4194304 | tf_op jit(solution)/shard_map/psum | solution.py:587
  258.8 9.3 %copy-start.31 = (bf16[1024,1408]{0,1:T(8,128)(2,1)S(1)}, bf16[1024,1408]{0,1:T(8,128)(2,1)}, u32[]{:S(2)}) copy-start(bf16[1024,1408]{0,1:T(8,128)(2,1)} %all-gather.11.cloned.1.call-done) | copy-start | bytes 8650756
  272.8 227.2 %reduce-scatter.11.cloned.1.call-start = ((), (), s32[]{:S(2)}) async-start(), calls=%async_computation.13 | async-start | bytes 1802240 | tf_op jit(solution)/shard_map/reduce_scatter | solution.py:502
  277.8 222.3 %reduce-scatter.7.cloned.1.call-start = ((), (), s32[]{:S(2)}) async-start(), calls=%async_computation.11 | async-start | bytes 1310720 | tf_op jit(solution)/shard_map/reduce_scatter | solution.py:502
  359.1 4.2 copy-start.2
  359.1 4.2 copy-start.3
  359.1 4.2 copy-start.10
  367.5 132.6 %reduce-scatter.9.cloned.1.call-start = ((), (), s32[]{:S(2)}) async-start(), calls=%async_computation.12 | async-start | bytes 3604480 | tf_op jit(solution)/shard_map/reduce_scatter | solution.py:502
  375.8 143.1 %reduce-scatter.5.cloned.1.call-start = ((), (), s32[]{:S(2)}) async-start(), calls=%async_computation.10 | async-start | bytes 3932160 | tf_op jit(solution)/shard_map/reduce_scatter | solution.py:502
  425.3 9.9 %collective-permute-start.2 = (f32[2,128,256]{2,1,0:T(8,128)}, f32[2,128,256]{2,1,0:T(8,128)S(1)}, u32[]{:S(2)}, u32[]{:S(2)}) collective-permute-start(f32[2,128,256]{2,1,0:T(8,128)} %delta_back_chain.1), channel_id=1, source_target_pairs={{4,0},{5,1},{6,2},{7,3},{12,8},{13,9},{14,10},{15,11},{20,16},{21,... | collective-permute-start | bytes 786440 | tf_op jit(solution)/shard_map/ppermute | solution.py:596
  468.0 6.2 collective-permute-start.3
  482.5 194.5 %all-reduce.13.cloned.1.call-start = ((), (), s32[]{:S(2)}) async-start(), calls=%async_computation.14 | async-start | bytes 8388608 | tf_op jit(solution)/shard_map/psum | solution.py:578
  484.1 5.0 copy-start.11
  498.8 245.4 %all-reduce.15.cloned.1.call-start = ((), (), s32[]{:S(2)}) async-start(), calls=%async_computation.15 | async-start | bytes 4259840 | tf_op jit(solution)/shard_map/psum | solution.py:503
  500.0 19.0 %copy-start.22 = (f32[8,1024]{1,0:T(8,128)S(1)}, f32[8,1024]{1,0:T(8,128)}, u32[]{:S(2)}) copy-start(f32[8,1024]{1,0:T(8,128)} %get-tuple-element.46) | copy-start | bytes 98308
  744.2 4.1 copy-start.17
  744.2 4.9 copy-start.14
  746.0 3.9 copy-start.9
  (20 other events, 34.6 us)
Sparse Core Ops, SparseCore 0:
  10.2 31.2 all-gather.6
  43.1 16.7 all-gather.8
  124.6 85.1 all-reduce.8
  211.8 26.4 all-gather.10
  239.7 19.0 all-gather.12
  273.0 86.1 all-reduce.10
  361.7 26.2 reduce-scatter.10
  390.5 24.8 reduce-scatter.6
  417.9 36.1 reduce-scatter.8
  482.7 36.2 reduce-scatter.4
  521.9 155.0 all-reduce.12
  679.3 64.8 all-reduce.14

commit v2 on v1

--- a/solution.py
+++ b/solution.py
@@ -4,6 +4,7 @@
 from jax import lax
 from jax.experimental import pallas as pl
 from jax.experimental.pallas import tpu as pltpu
+from jax.sharding import PartitionSpec as P
 
 F32 = jnp.float32
 BF16 = jnp.bfloat16
@@ -79,12 +80,28 @@
     return part, lax.rsqrt(jnp.sum(part * part, axis=1, keepdims=True) + EPSILON)
 
 
+AUX = 16
+FACTS = 5
+
+
+def rates(heads, lin, facts):
+    lane = lax.broadcasted_iota(jnp.int32, lin.shape, 1)
+    sig = jax.nn.sigmoid(lin)
+    soft = jnp.maximum(lin, 0.0) + jnp.log1p(jnp.exp(-jnp.abs(lin)))
+    main = jnp.where(lane < heads, sig, -soft).astype(BF16).astype(F32)[:, : 2 * heads]
+    slope = jnp.where(lane < heads, sig * (1.0 - sig), -sig)[:, : 2 * heads]
+    rest = AUX - 4 * heads - facts.shape[1]
+    pad = jnp.zeros((lin.shape[0], rest), F32)
+    return jnp.concatenate([main, facts, slope, pad], axis=1)
+
+
 def prepare_kernel(
-    sizes, raw_ref, halo_ref, aux_ref, taps_ref,
-    unit_ref, val_ref, inv_ref, wu_ref, mix_ref, just_ref, state_ref, ext_ref,
+    sizes, raw_ref, halo_ref, lin_ref, bias_ref, facts_ref, taps_ref,
+    unit_ref, val_ref, inv_ref, wu_ref, mix_ref, just_ref, state_ref, aux_ref, ext_ref,
 ):
     heads, dk, dv = sizes
     size = raw_ref.shape[0]
+    aux_ref[...] = rates(heads, lin_ref[...] + bias_ref[...], facts_ref[...])
 
     @pl.when(pl.program_id(0) == 0)
     def _():
@@ -141,7 +158,7 @@
         state_ref[h] = carried[size - 1 :, :] * state + mm(low, deep)
 
 
-def prepare(sizes, raw, halo, aux, taps):
+def prepare(sizes, raw, halo, gates, bias, facts, taps):
     heads, dk, dv = sizes
     span, width = raw.shape
     blocks = span // CHUNK
@@ -151,13 +168,17 @@
     return pl.pallas_call(
         functools.partial(prepare_kernel, sizes),
         grid=(blocks,),
-        in_specs=[rowed(width), fixed(halo), rowed(aux.shape[1]), fixed(taps)],
+        in_specs=[
+            rowed(width), fixed(halo), pl.BlockSpec((c, 128), lambda i: (i, heads * dv // 128)),
+            fixed(bias), rowed(facts.shape[1]), fixed(taps),
+        ],
         out_specs=[
             rowed(2 * heads * dk), rowed(heads * dv), rowed(heads * c),
             rowed(heads * (dk + dv)),
             pl.BlockSpec((1, heads, c + dk, c + dk), lambda i: (i, 0, 0, 0)),
             rowed(heads * c),
             pl.BlockSpec((heads, dk, dv), lambda i: (0, 0, 0)),
+            rowed(AUX),
         ],
         out_shape=[
             jax.ShapeDtypeStruct((span, 2 * heads * dk), BF16),
@@ -167,33 +188,44 @@
             jax.ShapeDtypeStruct((blocks, heads, c + dk, c + dk), BF16),
             jax.ShapeDtypeStruct((span, heads * c), BF16),
             jax.ShapeDtypeStruct((heads, dk, dv), F32),
+            jax.ShapeDtypeStruct((span, AUX), F32),
         ],
         scratch_shapes=[pltpu.VMEM((c + 8, width), F32)],
         name="delta_prepare",
-    )(raw, halo, aux, taps)
-
-
-def apply_kernel(sizes, mix_ref, wu_ref, aux_ref, start_ref, out_ref, states_ref, state_ref):
+    )(raw, halo, gates, bias, facts, taps)
+
+
+def through_of(heads, aux, h):
+    decay = aux[:, heads + h : heads + h + 1]
+    before = aux[aux.shape[0] - 1 :, 2 * heads + 1 : 2 * heads + 2]
+    return before * jnp.exp(jnp.sum(decay, axis=0, keepdims=True))
+
+
+def apply_step(sizes, aux, mix_ref, wu_ref, states_ref, state_ref):
     heads, dk, dv = sizes
     size = wu_ref.shape[0]
-
-    @pl.when(pl.program_id(0) == 0)
-    def _():
-        state_ref[...] = start_ref[...]
-
-    aux = aux_ref[...]
+    outs = []
     for h in range(heads):
-        decay = aux[:, heads + h : heads + h + 1]
-        before = aux[size - 1 :, 2 * heads + 1 : 2 * heads + 2]
-        through = before * jnp.exp(jnp.sum(decay, axis=0, keepdims=True))
         state = state_ref[h]
         low = state.astype(BF16)
         states_ref[0, h] = low
         first = h * (dk + dv) + dk
         deep = jnp.concatenate([low, wu_ref[:, first : first + dv]], axis=0)
         both = mm(mix_ref[0, h], deep)
-        out_ref[:, h * dv : (h + 1) * dv] = both[:size].astype(BF16)
-        state_ref[h] = through * state + both[size:]
+        outs.append(both[:size].astype(BF16))
+        state_ref[h] = through_of(heads, aux, h) * state + both[size:]
+    return outs
+
+
+def apply_kernel(sizes, mix_ref, wu_ref, aux_ref, start_ref, out_ref, states_ref, state_ref):
+    @pl.when(pl.program_id(0) == 0)
+    def _():
+        state_ref[...] = start_ref[...]
+
+    dv = sizes[2]
+    outs = apply_step(sizes, aux_ref[...], mix_ref, wu_ref, states_ref, state_ref)
+    for h, out in enumerate(outs):
+        out_ref[:, h * dv : (h + 1) * dv] = out
 
 
 def apply_states(sizes, mix, wu, aux, start):
@@ -224,24 +256,23 @@
     )(mix, wu, aux, start)
 
 
+def back_chain_step(sizes, aux, mix_ref, grads, state_ref):
+    heads, dk, _ = sizes
+    for h in range(heads):
+        state = state_ref[h]
+        deep = jnp.concatenate([grads[h], state.astype(BF16)], axis=0)
+        state_ref[h] = through_of(heads, aux, h) * state + mm(mix_ref[0, h, :, 0:dk], deep, TN)
+
+
 def back_chain_kernel(sizes, mix_ref, grad_ref, aux_ref, end_ref, state_ref):
     heads, dk, dv = sizes
-    size = grad_ref.shape[0]
 
     @pl.when(pl.program_id(0) == 0)
     def _():
         state_ref[...] = end_ref[...]
 
-    aux = aux_ref[...]
-    for h in range(heads):
-        decay = aux[:, heads + h : heads + h + 1]
-        before = aux[size - 1 :, 2 * heads + 1 : 2 * heads + 2]
-        through = before * jnp.exp(jnp.sum(decay, axis=0, keepdims=True))
-        state = state_ref[h]
-        deep = jnp.concatenate(
-            [grad_ref[:, h * dv : (h + 1) * dv], state.astype(BF16)], axis=0
-        )
-        state_ref[h] = through * state + mm(mix_ref[0, h, :, 0:dk], deep, TN)
+    grads = [grad_ref[:, h * dv : (h + 1) * dv] for h in range(heads)]
+    back_chain_step(sizes, aux_ref[...], mix_ref, grads, state_ref)
 
 
 def back_chain(sizes, mix, grad, aux, end):
@@ -268,7 +299,7 @@
 def back_kernel(
     sizes, raw_ref, prev_ref, halo_ref, aux_ref, taps_ref, unit_ref, val_ref, inv_ref, wu_ref,
     mix_ref, just_ref, states_ref, grad_ref, end_ref,
-    draw_ref, tail_ref, head_ref, dtaps_ref, daux_ref,
+    draw_ref, tail_ref, head_ref, dtaps_ref, daux_ref, dbias_ref,
     state_ref, ext_ref, next_ref, zext_ref, dsil_ref,
 ):
     heads, dk, dv = sizes
@@ -281,6 +312,7 @@
         state_ref[...] = end_ref[...]
         next_ref[...] = jnp.zeros_like(next_ref)
         dtaps_ref[...] = jnp.zeros_like(dtaps_ref)
+        dbias_ref[...] = jnp.zeros_like(dbias_ref)
 
     @pl.when(step == steps - 1)
     def _():
@@ -366,8 +398,10 @@
         dtotal = dtotal + jnp.where(is_last, jnp.sum(kz, axis=0, keepdims=True), 0.0)
         dtotal_row = to_row(dtotal, eye) - jnp.sum(flow, axis=0, keepdims=True)
         ddecay = jnp.sum(jnp.where(cols >= rows, dtotal_row, 0.0), axis=1, keepdims=True)
-        daux = daux + jnp.where(lanes == h, dbeta, 0.0)
-        daux = daux + jnp.where(lanes == heads + h, ddecay, 0.0)
+        slope = 2 * heads + FACTS + h
+        daux = daux + jnp.where(lanes == h, dbeta * aux[:, slope : slope + 1], 0.0)
+        slope = slope + heads
+        daux = daux + jnp.where(lanes == heads + h, ddecay * aux[:, slope : slope + 1], 0.0)
         dsil_ref[:, 2 * heads * dk + h * dv : 2 * heads * dk + (h + 1) * dv] = beta * dres
         for first, grad, scale in ((h, dquery, dk ** (-0.5)), (heads + h, dkey, 1.0)):
             part, norm = unit_parts(silu, first * dk, dk)
@@ -375,7 +409,8 @@
             grad = grad * scale
             inner = jnp.sum(unit * grad, axis=1, keepdims=True)
             dsil_ref[:, first * dk : (first + 1) * dk] = norm * (grad - unit * inner)
-    daux_ref[...] = daux
+    daux_ref[...] = daux.astype(BF16)
+    dbias_ref[0:1, :] += jnp.sum(daux, axis=0, keepdims=True)
     dconv = dsil_ref[...] * (sig * (1.0 + conv * (1.0 - sig)))
     draw = dconv * taps[0:1, :]
     dtaps_ref[0:1, :] += jnp.sum(dconv * x, axis=0, keepdims=True)
@@ -430,14 +465,16 @@
             rowed(heads * dv), fixed(end.shape),
         ],
         out_specs=[
-            rowed(width), fixed((8, width)), fixed((8, width)), fixed((8, width)), rowed(8),
+            rowed(width), fixed((8, width)), fixed((8, width)), fixed((8, width)), rowed(128),
+            fixed((8, 128)),
         ],
         out_shape=[
             jax.ShapeDtypeStruct((span, width), BF16),
             jax.ShapeDtypeStruct((8, width), F32),
             jax.ShapeDtypeStruct((8, width), F32),
             jax.ShapeDtypeStruct((8, width), F32),
-            jax.ShapeDtypeStruct((span, 8), F32),
+            jax.ShapeDtypeStruct((span, 128), BF16),
+            jax.ShapeDtypeStruct((8, 128), F32),
         ],
         scratch_shapes=[
             pltpu.VMEM((heads, dk, dv), F32),
@@ -450,7 +487,630 @@
     )(raw, raw, halo, aux, taps, unit, val, inv, wu, mix, just, states, grad, end)
 
 
-from jax.sharding import PartitionSpec as P
+MESH = pl.DeviceIdType.MESH
+SPAN = 128
+PIECES = 2
+
+
+def line_roles():
+    spot = lax.axis_index("tp")
+    middle = (spot == 1) | (spot == 2)
+    near = jnp.where(spot < 2, 1 - spot, 5 - spot)
+    half = jnp.where(spot == 1, 0, 1)
+    return middle, near, 3 - spot, half
+
+
+def enter(grid_peers):
+    middle, near, other, _ = line_roles()
+    barrier = pltpu.get_barrier_semaphore()
+    pl.semaphore_signal(barrier, inc=1, device_id={"tp": near}, device_id_type=MESH)
+    waits = 1
+    if grid_peers:
+        for peer in grid_devices():
+            pl.semaphore_signal(barrier, inc=1, device_id=peer, device_id_type=MESH)
+            waits += 1
+
+    @pl.when(middle)
+    def _():
+        pl.semaphore_signal(barrier, inc=1, device_id={"tp": other}, device_id_type=MESH)
+
+    pl.semaphore_wait(barrier, waits + jnp.where(middle, 1, 0))
+
+
+def grid_devices():
+    shard, ctx = lax.axis_index("shard"), lax.axis_index("ctx")
+    shards, ctxs = lax.axis_size("shard"), lax.axis_size("ctx")
+    peers = []
+    for ds in range(shards):
+        for dc in range(ctxs):
+            if ds or dc:
+                peers.append({"shard": (shard + ds) % shards, "ctx": (ctx + dc) % ctxs})
+    return peers
+
+
+class LineSum:
+    def __init__(self, count, own, rece, cross, recm, fin, sem):
+        self.count = count
+        self.own, self.rece, self.cross, self.recm, self.fin = own, rece, cross, recm, fin
+        self.sem = sem
+        self.middle, self.near, self.other, self.half = line_roles()
+
+    def copy(self, src, dst, kind, piece, device):
+        return pltpu.make_async_remote_copy(
+            src_ref=src, dst_ref=dst, send_sem=self.sem.at[0, kind, piece],
+            recv_sem=self.sem.at[1, kind, piece], device_id={"tp": device}, device_id_type=MESH,
+        )
+
+    def up(self, k):
+        return self.copy(self.own.at[k], self.rece.at[k], 0, k, self.near)
+
+    def over(self, k):
+        return self.copy(self.cross.at[k], self.recm.at[k], 1, k, self.other)
+
+    def final(self, k, kind, half, device):
+        place = self.fin.at[k, half]
+        return self.copy(place, place, kind, k, device)
+
+    def when(self, k, low, high, what):
+        pl.when((k >= low) & (k < high))(what)
+
+    def advance(self, k):
+        count = self.count
+        mine, theirs = self.half, 1 - self.half
+
+        @pl.when(jnp.logical_not(self.middle) & (k < count))
+        def _():
+            self.up(k).start()
+
+        @pl.when(self.middle & (k >= 2) & (k < count + 2))
+        def _():
+            j = k - 2
+            self.up(j).wait_recv()
+            total = self.own[j, theirs].astype(F32) + self.rece[j, theirs].astype(F32)
+            self.cross[j] = total.astype(BF16)
+            self.over(j).start()
+
+        @pl.when(self.middle & (k >= 3) & (k < count + 3))
+        def _():
+            j = k - 3
+            self.over(j).wait_recv()
+            total = self.own[j, mine].astype(F32) + self.rece[j, mine].astype(F32)
+            self.fin[j, mine] = (total + self.recm[j].astype(F32)).astype(BF16)
+            self.final(j, 2, mine, self.other).start()
+            self.final(j, 3, mine, self.near).start()
+
+        @pl.when(self.middle & (k >= 4) & (k < count + 4))
+        def _():
+            j = k - 4
+            self.final(j, 2, theirs, self.other).wait_recv()
+            self.final(j, 4, theirs, self.near).start()
+
+    def arrive(self, k):
+        @pl.when(jnp.logical_not(self.middle))
+        def _():
+            self.final(k, 3, 0, self.near).wait_recv()
+            self.final(k, 4, 0, self.near).wait_recv()
+
+    def drain(self):
+        def step(k, carry):
+            @pl.when(self.middle)
+            def _():
+                self.over(k).wait_send()
+                self.final(k, 2, self.half, self.other).wait_send()
+                self.final(k, 3, self.half, self.near).wait_send()
+                self.final(k, 4, 1 - self.half, self.near).wait_send()
+
+            @pl.when(jnp.logical_not(self.middle))
+            def _():
+                self.up(k).wait_send()
+
+            return carry
+
+        lax.fori_loop(0, self.count, step, 0)
+
+
+def line_scratch(count, rows, width):
+    half = rows // 2
+    return [
+        pltpu.VMEM((count, 2, half, width), BF16),
+        pltpu.VMEM((count, 2, half, width), BF16),
+        pltpu.VMEM((count, half, width), BF16),
+        pltpu.VMEM((count, half, width), BF16),
+        pltpu.VMEM((count, 2, half, width), BF16),
+        pltpu.SemaphoreType.DMA((2, 5, count)),
+    ]
+
+
+LAG = 3
+
+
+class ShardSum:
+    def __init__(self, parts, axes, bufs, sem):
+        self.parts, self.axes, self.bufs, self.sem = parts, axes, bufs, sem
+        self.shard, self.ctx = lax.axis_index("shard"), lax.axis_index("ctx")
+        self.ctxs = lax.axis_size("ctx")
+        self.core, self.row = self.shard % 2, self.shard // 2
+
+    def block(self, item, owner):
+        ref, axis = self.parts[item], self.axes[item]
+        size = ref.shape[axis] // 4
+        cut = pl.ds(pl.multiple_of(owner * size, size), size)
+        return ref.at[cut, :] if axis == 0 else ref.at[:, cut]
+
+    def copy(self, src, dst, item, kind, device):
+        return pltpu.make_async_remote_copy(
+            src_ref=src, dst_ref=dst, send_sem=self.sem.at[0, item, kind],
+            recv_sem=self.sem.at[1, item, kind], device_id=device, device_id_type=MESH,
+        )
+
+    def swap(self, item, row):
+        heard = self.bufs[item][0]
+        return self.copy(
+            self.block(item, 2 * row + 1 - self.core), heard.at[row], item, row,
+            {"shard": 2 * self.row + 1 - self.core},
+        )
+
+    def along(self, item):
+        _, added, heard, _, _ = self.bufs[item]
+        return self.copy(
+            added.at[1], heard, item, 2, {"shard": 2 * (1 - self.row) + self.core}
+        )
+
+    def across(self, item, distance):
+        _, _, _, total, slots = self.bufs[item]
+        peer = (self.ctx + distance) % self.ctxs
+        return self.copy(total, slots.at[distance], item, 2 + distance, {"ctx": peer})
+
+    def first(self):
+        for item in range(len(self.parts)):
+            for row in range(2):
+                self.swap(item, row).start()
+
+    def second(self, item):
+        heard, added, _, _, _ = self.bufs[item]
+        for row in range(2):
+            self.swap(item, row).wait_recv()
+        for place, row in ((1, 1 - self.row), (0, self.row)):
+            mine = self.block(item, 2 * row + self.core)[...].astype(F32)
+            added[place] = (mine + heard[row].astype(F32)).astype(BF16)
+            if place:
+                self.along(item).start()
+
+    def third(self, item):
+        _, added, heard, total, _ = self.bufs[item]
+        self.along(item).wait_recv()
+        total[...] = (added[0].astype(F32) + heard[...].astype(F32)).astype(BF16)
+        for distance in range(1, self.ctxs):
+            self.across(item, distance).start()
+
+    def last(self, item):
+        _, _, _, total, slots = self.bufs[item]
+        for distance in range(1, self.ctxs):
+            self.across(item, distance).wait_recv()
+        if self.ctxs == 2:
+            return total[...].astype(F32) + slots[1].astype(F32)
+        result = None
+        for rank in range(self.ctxs):
+            gap = (self.ctx - rank) % self.ctxs
+            term = jnp.where(
+                gap == 0, total[...].astype(F32), slots[jnp.maximum(gap, 1)].astype(F32)
+            )
+            result = term if result is None else result + term
+        return result
+
+    def drain(self, item):
+        for row in range(2):
+            self.swap(item, row).wait_send()
+        self.along(item).wait_send()
+        for distance in range(1, self.ctxs):
+            self.across(item, distance).wait_send()
+
+
+def shard_blocks(parts, axes):
+    blocks = []
+    for part, axis in zip(parts, axes):
+        rows, cols = part.shape
+        blocks.append((rows // 4, cols) if axis == 0 else (rows, cols // 4))
+    return blocks
+
+
+def shard_scratch(blocks, ctxs):
+    bufs = []
+    for block in blocks:
+        bufs += [
+            pltpu.VMEM((2,) + block, BF16), pltpu.VMEM((2,) + block, BF16),
+            pltpu.VMEM(block, BF16), pltpu.VMEM(block, BF16),
+            pltpu.VMEM((ctxs,) + block, BF16),
+        ]
+    return bufs + [pltpu.SemaphoreType.DMA((2, len(blocks), 2 + ctxs))]
+
+
+def pieces_of(total):
+    return total.astype(BF16).reshape(PIECES, 2, SPAN // PIECES // 2, total.shape[1])
+
+
+def normalise(vector):
+    rate = lax.rsqrt(jnp.mean(vector * vector, axis=1, keepdims=True) + EPSILON)
+    return vector * rate, rate
+
+
+def norm_back(unit, rate, grad):
+    return rate * (grad - unit * jnp.mean(grad * unit, axis=1, keepdims=True))
+
+
+def out_kernel(
+    sizes, blocks, mix_ref, wu_ref, aux_ref, start_ref, gate_ref, gain_ref, weight_ref, tokens_ref,
+    gain_two_ref, mixed_ref, states_ref, gated_ref, hidden_ref, normed_ref,
+    state_ref, own, rece, cross, recm, fin, sem,
+):
+    heads, dk, dv = sizes
+    line = LineSum(blocks * PIECES, own, rece, cross, recm, fin, sem)
+    step = pl.program_id(0)
+
+    @pl.when(step == 0)
+    def _():
+        state_ref[...] = start_ref[...]
+        enter(False)
+
+    @pl.when(step < blocks)
+    def _():
+        aux = aux_ref[...]
+        outs = apply_step(sizes, aux, mix_ref, wu_ref, states_ref, state_ref)
+        live = jnp.where(aux[:, 2 * heads : 2 * heads + 1] >= 0.0, 1.0, 0.0)
+        parts = []
+        for h, out in enumerate(outs):
+            cut = slice(h * dv, (h + 1) * dv)
+            mixed_ref[:, cut] = out
+            unit, _ = normalise(out.astype(F32))
+            gate = gate_ref[:, cut]
+            gated = unit * gain_ref[:, cut] * (gate * jax.nn.sigmoid(gate)) * live
+            parts.append(gated.astype(BF16))
+        gated = jnp.concatenate(parts, axis=1)
+        gated_ref[...] = gated
+        own[pl.ds(step * PIECES, PIECES)] = pieces_of(mm(gated, weight_ref[...]))
+
+    for piece in range(PIECES):
+        line.advance(step * PIECES + piece)
+
+    @pl.when(step >= LAG)
+    def _():
+        for piece in range(PIECES):
+            line.arrive((step - LAG) * PIECES + piece)
+        attended = fin[pl.ds((step - LAG) * PIECES, PIECES)].reshape(hidden_ref.shape)
+        hidden = tokens_ref[...].astype(F32) + attended.astype(F32)
+        hidden_ref[...] = hidden
+        normed_ref[...] = (normalise(hidden)[0] * gain_two_ref[...]).astype(BF16)
+
+    @pl.when(step == blocks + LAG - 1)
+    def _():
+        line.drain()
+
+
+def out_sum(sizes, mix, wu, aux, start, gates, gain, weight, tokens, gain_two):
+    heads, dk, dv = sizes
+    rows, width = tokens.shape
+    blocks = rows // SPAN
+    c = SPAN
+    early = lambda i: jnp.minimum(i, blocks - 1)
+    late = lambda i: jnp.maximum(i - LAG, 0)
+    rowed = lambda w: pl.BlockSpec((c, w), lambda i: (early(i), 0))
+    after = lambda w: pl.BlockSpec((c, w), lambda i: (late(i), 0))
+    fixed = lambda a: pl.BlockSpec(
+        a.shape, lambda i: (0,) * a.ndim, pipeline_mode=pl.Buffered(1)
+    )
+    return pl.pallas_call(
+        functools.partial(out_kernel, sizes, blocks),
+        grid=(blocks + LAG,),
+        in_specs=[
+            pl.BlockSpec((1, heads, c + dk, c + dk), lambda i: (early(i), 0, 0, 0)),
+            rowed(wu.shape[1]), rowed(aux.shape[1]), fixed(start), rowed(heads * dv),
+            fixed(gain), fixed(weight), after(width), fixed(gain_two),
+        ],
+        out_specs=[
+            rowed(heads * dv),
+            pl.BlockSpec((1, heads, dk, dv), lambda i: (early(i), 0, 0, 0)),
+            rowed(heads * dv), after(width), after(width),
+        ],
+        out_shape=[
+            jax.ShapeDtypeStruct((rows, heads * dv), BF16),
+            jax.ShapeDtypeStruct((blocks, heads, dk, dv), BF16),
+            jax.ShapeDtypeStruct((rows, heads * dv), BF16),
+            jax.ShapeDtypeStruct((rows, width), F32),
+            jax.ShapeDtypeStruct((rows, width), BF16),
+        ],
+        scratch_shapes=[pltpu.VMEM((heads, dk, dv), F32)]
+        + line_scratch(blocks * PIECES, SPAN // PIECES, width),
+        compiler_params=pltpu.CompilerParams(collective_id=1, has_side_effects=True),
+        cost_estimate=pl.CostEstimate(
+            flops=4_000_000_000, bytes_accessed=150_000_000, transcendentals=0
+        ),
+        name="out_sum",
+    )(mix, wu, aux, start, gates, gain, weight, tokens, gain_two)
+
+
+def run_shard_sum(grid_sum, step, outs, starts):
+    second, third, last = starts
+    for item, (one, two, three) in enumerate(zip(second, third, last)):
+
+        @pl.when(step == one)
+        def _():
+            grid_sum.second(item)
+
+        @pl.when(step == two)
+        def _():
+            grid_sum.third(item)
+
+        @pl.when(step == three)
+        def _():
+            result = grid_sum.last(item)
+            first = 0
+            for out in outs[item]:
+                size = out.shape[1]
+                out[...] = result[:, first : first + size]
+                first += size
+            grid_sum.drain(item)
+
+
+def mlp_back_kernel(
+    sizes, blocks, axes, *refs,
+):
+    heads, dk, dv = sizes
+    items = len(axes)
+    (gate_up_a, gate_up_b, weight_a, weight_b, hidden_ref, cot_ref, mixed_ref, gates_ref, aux_ref,
+     mix_ref, out_w_ref, gain_ref, gain_two_ref), refs = refs[:13], refs[13:]
+    parts, refs = refs[:items], refs[items:]
+    (gh_ref, branch_ref, dmixed_ref, dgate_ref, state_ref, dgain_two_ref, dgain_ref), refs = (
+        refs[:7], refs[7:],
+    )
+    outs, refs = refs[:items], refs[items:]
+    (own, rece, cross, recm, fin, sem), refs = refs[:6], refs[6:]
+    bufs = [refs[5 * i : 5 * i + 5] for i in range(items)]
+    grid_sum = ShardSum(parts, axes, bufs, refs[5 * items])
+    line = LineSum(blocks * PIECES, own, rece, cross, recm, fin, sem)
+    step = pl.program_id(0)
+
+    @pl.when(step == 0)
+    def _():
+        state_ref[...] = jnp.zeros_like(state_ref)
+        dgain_two_ref[...] = jnp.zeros_like(dgain_two_ref)
+        dgain_ref[...] = jnp.zeros_like(dgain_ref)
+        enter(True)
+        grid_sum.first()
+
+    @pl.when(step < blocks)
+    def _():
+        total = mm(gate_up_a[...], weight_a[...], NT) + mm(gate_up_b[...], weight_b[...], NT)
+        own[pl.ds(step * PIECES, PIECES)] = pieces_of(total)
+
+    for piece in range(PIECES):
+        line.advance(step * PIECES + piece)
+    run_shard_sum(grid_sum, step, [[o] for o in outs], ((1, 1, 2), (4, 6, 8), (10, 10, 10)))
+
+    @pl.when(step >= LAG)
+    def _():
+        for piece in range(PIECES):
+            line.arrive((step - LAG) * PIECES + piece)
+        grad = fin[pl.ds((step - LAG) * PIECES, PIECES)].reshape(gh_ref.shape).astype(F32)
+        unit, rate = normalise(hidden_ref[...])
+        dgain_two_ref[0:1, :] += jnp.sum(grad * unit, axis=0, keepdims=True)
+        grad = cot_ref[...].astype(F32) + norm_back(unit, rate, grad * gain_two_ref[...])
+        gh_ref[...] = grad
+        branch = grad.astype(BF16)
+        branch_ref[...] = branch
+        aux = aux_ref[...]
+        live = jnp.where(aux[:, 2 * heads : 2 * heads + 1] >= 0.0, 1.0, 0.0)
+        dgated = mm(branch, out_w_ref[...], NT) * live
+        dmixed = []
+        for h in range(heads):
+            cut = slice(h * dv, (h + 1) * dv)
+            unit, rate = normalise(mixed_ref[:, cut].astype(F32))
+            gate = gates_ref[:, cut]
+            sig = jax.nn.sigmoid(gate)
+            gain = gain_ref[:, cut]
+            part = dgated[:, cut]
+            flow = part * (gate * sig)
+            dgain_ref[0:1, cut] += jnp.sum(flow * unit, axis=0, keepdims=True)
+            low = norm_back(unit, rate, flow * gain).astype(BF16)
+            dmixed_ref[:, cut] = low
+            dmixed.append(low)
+            slope = sig * (1.0 + gate * (1.0 - sig))
+            dgate_ref[:, cut] = (part * (unit * gain) * slope).astype(BF16)
+        back_chain_step(sizes, aux, mix_ref, dmixed, state_ref)
+
+    @pl.when(step == blocks + LAG - 1)
+    def _():
+        line.drain()
+
+
+def mlp_back_sum(
+    sizes, dgate, dup, gate_w, up_w, hidden, cot, mixed, gates, aux, mix, out_w, gain, gain_two,
+    parts, axes,
+):
+    heads, dk, dv = sizes
+    rows, width = cot.shape
+    blocks = rows // SPAN
+    top = blocks - 1
+    c = SPAN
+    early = lambda i: top - jnp.minimum(i, top)
+    late = lambda i: top - jnp.maximum(i - LAG, 0)
+    rowed = lambda w: pl.BlockSpec((c, w), lambda i: (early(i), 0))
+    after = lambda w: pl.BlockSpec((c, w), lambda i: (late(i), 0))
+    whole = lambda shape: pl.BlockSpec(
+        shape, lambda i: (0,) * len(shape), pipeline_mode=pl.Buffered(1)
+    )
+    keep = lambda shape: pl.BlockSpec(shape, lambda i: (0,) * len(shape))
+    owned = shard_blocks(parts, axes)
+    units = gate_w.shape[1]
+    return pl.pallas_call(
+        functools.partial(mlp_back_kernel, sizes, blocks, axes),
+        grid=(blocks + LAG,),
+        in_specs=[
+            rowed(units), rowed(units), whole(gate_w.shape), whole(up_w.shape), after(width),
+            after(width), after(heads * dv), after(heads * dv), after(aux.shape[1]),
+            pl.BlockSpec((1, heads, c + dk, c + dk), lambda i: (late(i), 0, 0, 0)),
+            whole(out_w.shape), whole(gain.shape), whole(gain_two.shape),
+        ]
+        + [whole(p.shape) for p in parts],
+        out_specs=[
+            after(width), after(width), after(heads * dv), after(heads * dv),
+            keep((heads, dk, dv)), keep((8, width)), keep((8, heads * dv)),
+        ]
+        + [keep(b) for b in owned],
+        out_shape=[
+            jax.ShapeDtypeStruct((rows, width), F32),
+            jax.ShapeDtypeStruct((rows, width), BF16),
+            jax.ShapeDtypeStruct((rows, heads * dv), BF16),
+            jax.ShapeDtypeStruct((rows, heads * dv), BF16),
+            jax.ShapeDtypeStruct((heads, dk, dv), F32),
+            jax.ShapeDtypeStruct((8, width), F32),
+            jax.ShapeDtypeStruct((8, heads * dv), F32),
+        ]
+        + [jax.ShapeDtypeStruct(b, F32) for b in owned],
+        scratch_shapes=line_scratch(blocks * PIECES, SPAN // PIECES, width)
+        + shard_scratch(owned, lax.axis_size("ctx")),
+        compiler_params=pltpu.CompilerParams(collective_id=2, has_side_effects=True),
+        cost_estimate=pl.CostEstimate(
+            flops=6_000_000_000, bytes_accessed=150_000_000, transcendentals=0
+        ),
+        name="mlp_back_sum",
+    )(
+        dgate, dup, gate_w, up_w, hidden, cot, mixed, gates, aux, mix, out_w, gain, gain_two,
+        *parts,
+    )
+
+
+class TinySum:
+    def __init__(self, shares, slots, sem):
+        self.shares, self.slots, self.sem = shares, slots, sem
+        self.shard, self.ctx = lax.axis_index("shard"), lax.axis_index("ctx")
+        self.shards, self.ctxs = lax.axis_size("shard"), lax.axis_size("ctx")
+
+    def copy(self, index, device):
+        me = self.shard * self.ctxs + self.ctx
+        return pltpu.make_async_remote_copy(
+            src_ref=self.shares.at[device["shard"]], dst_ref=self.slots.at[me],
+            send_sem=self.sem.at[0, index], recv_sem=self.sem.at[1, index],
+            device_id=device, device_id_type=MESH,
+        )
+
+    def run(self):
+        me = self.shard * self.ctxs + self.ctx
+        self.slots[me] = self.shares[self.shard]
+        copies = [self.copy(i, device) for i, device in enumerate(grid_devices())]
+        for copy in copies:
+            copy.start()
+        for copy in copies:
+            copy.wait()
+        total = self.slots[0]
+        for index in range(1, self.shards * self.ctxs):
+            total = total + self.slots[index]
+        return total
+
+
+def mixer_back_kernel(sizes, blocks, axes, cuts, *refs):
+    items = len(axes)
+    (draw_ref, dgate_ref, dsmall_ref, weight_ref, tokens_ref, gh_ref, gain_ref, tiny_ref), refs = (
+        refs[:8], refs[8:],
+    )
+    parts, refs = refs[:items], refs[items:]
+    (grad_ref, tiny_out), refs = refs[:2], refs[2:]
+    outs = []
+    for cut in cuts:
+        outs.append(refs[:cut])
+        refs = refs[cut:]
+    (own, rece, cross, recm, fin, sem), refs = refs[:6], refs[6:]
+    bufs = [refs[5 * i : 5 * i + 5] for i in range(items)]
+    grid_sum = ShardSum(parts, axes, bufs, refs[5 * items])
+    dgain_ref, shares, slots, tiny_sem = refs[5 * items + 1 :]
+    line = LineSum(blocks * PIECES, own, rece, cross, recm, fin, sem)
+    step = pl.program_id(0)
+    wide = draw_ref.shape[1]
+    gated = dgate_ref.shape[1]
+
+    @pl.when(step == 0)
+    def _():
+        dgain_ref[...] = jnp.zeros_like(dgain_ref)
+        enter(True)
+        grid_sum.first()
+
+    @pl.when(step < blocks)
+    def _():
+        total = mm(draw_ref[...], weight_ref[:, :wide], NT)
+        total = total + mm(dgate_ref[...], weight_ref[:, wide : wide + gated], NT)
+        total = total + mm(dsmall_ref[...], weight_ref[:, wide + gated :], NT)
+        own[pl.ds(step * PIECES, PIECES)] = pieces_of(total)
+
+    for piece in range(PIECES):
+        line.advance(step * PIECES + piece)
+    run_shard_sum(
+        grid_sum, step, outs, ((1, 1, 2, 2), (4, 6, 6, 8), (8, 10, 10, 10))
+    )
+
+    @pl.when(step >= LAG)
+    def _():
+        for piece in range(PIECES):
+            line.arrive((step - LAG) * PIECES + piece)
+        grad = fin[pl.ds((step - LAG) * PIECES, PIECES)].reshape(grad_ref.shape).astype(F32)
+        unit, rate = normalise(tokens_ref[...].astype(F32))
+        dgain_ref[0:1, :] += jnp.sum(grad * unit, axis=0, keepdims=True)
+        grad_ref[...] = gh_ref[...] + norm_back(unit, rate, grad * gain_ref[...])
+
+    @pl.when(step == blocks + LAG - 1)
+    def _():
+        shares[...] = tiny_ref[...]
+        share = dgain_ref.shape[1] // 4
+        for owner in range(4):
+            for line_at in range(share // 128):
+                first = owner * share + line_at * 128
+                shares[owner, line_at : line_at + 1, :] = dgain_ref[0:1, first : first + 128]
+        tiny_out[...] = TinySum(shares, slots, tiny_sem).run()
+        line.drain()
+
+
+def mixer_back_sum(sizes, draw, dgate, dsmall, weight, tokens, gh, gain, tiny, parts, axes, splits):
+    rows, width = tokens.shape
+    blocks = rows // SPAN
+    c = SPAN
+    early = lambda i: jnp.minimum(i, blocks - 1)
+    late = lambda i: jnp.maximum(i - LAG, 0)
+    rowed = lambda w: pl.BlockSpec((c, w), lambda i: (early(i), 0))
+    after = lambda w: pl.BlockSpec((c, w), lambda i: (late(i), 0))
+    whole = lambda shape: pl.BlockSpec(
+        shape, lambda i: (0,) * len(shape), pipeline_mode=pl.Buffered(1)
+    )
+    keep = lambda shape: pl.BlockSpec(shape, lambda i: (0,) * len(shape))
+    owned = shard_blocks(parts, axes)
+    results = []
+    for block, split in zip(owned, splits):
+        results += [(block[0], w) for w in split]
+    devices = lax.axis_size("shard") * lax.axis_size("ctx")
+    return pl.pallas_call(
+        functools.partial(mixer_back_kernel, sizes, blocks, axes, [len(s) for s in splits]),
+        grid=(blocks + LAG,),
+        in_specs=[
+            rowed(draw.shape[1]), rowed(dgate.shape[1]), rowed(dsmall.shape[1]),
+            whole(weight.shape), after(width), after(width), whole(gain.shape), whole(tiny.shape),
+        ]
+        + [whole(p.shape) for p in parts],
+        out_specs=[after(width), keep(tiny.shape[1:])] + [keep(r) for r in results],
+        out_shape=[
+            jax.ShapeDtypeStruct((rows, width), F32),
+            jax.ShapeDtypeStruct(tiny.shape[1:], F32),
+        ]
+        + [jax.ShapeDtypeStruct(r, F32) for r in results],
+        scratch_shapes=line_scratch(blocks * PIECES, SPAN // PIECES, width)
+        + shard_scratch(owned, lax.axis_size("ctx"))
+        + [
+            pltpu.VMEM((8, width), F32), pltpu.VMEM(tiny.shape, F32),
+            pltpu.VMEM((devices,) + tiny.shape[1:], F32),
+            pltpu.SemaphoreType.DMA((2, devices - 1)),
+        ],
+        compiler_params=pltpu.CompilerParams(collective_id=3, has_side_effects=True),
+        cost_estimate=pl.CostEstimate(
+            flops=6_000_000_000, bytes_accessed=150_000_000, transcendentals=0
+        ),
+        name="mixer_back_sum",
+    )(draw, dgate, dsmall, weight, tokens, gh, gain, tiny, *parts)
 
 
 def dot_plain(left, right):
@@ -462,24 +1122,7 @@
 
 
 def dot_outer(left, right):
-    return lax.dot_general(left, right, TN, preferred_element_type=F32)
-
-
-def rms_norm(vector, scale_gain):
-    return (
-        vector * lax.rsqrt(jnp.mean(vector * vector, axis=-1, keepdims=True) + EPSILON) * scale_gain
-    )
-
-
-def gated_norm(mixed_in, gate_in, gain_in, live_rows):
-    head_count = gain_in.shape[0]
-    per_head = mixed_in.reshape(mixed_in.shape[0], head_count, -1)
-    gated_rows = rms_norm(per_head, gain_in) * jax.nn.silu(gate_in).reshape(per_head.shape)
-    return (gated_rows * live_rows[:, None, None]).reshape(mixed_in.shape)
-
-
-def gate_rates(beta_lin, decay_lin, bias_in):
-    return (jax.nn.sigmoid(beta_lin), -jax.nn.softplus(decay_lin + bias_in))
+    return lax.dot_general(left, right, TN, preferred_element_type=F32).astype(BF16)
 
 
 def row_facts(segment_ids, first, span):
@@ -494,13 +1137,7 @@
     here = at(0)
     before = jnp.repeat(at(1).reshape(-1, CHUNK)[:, 0], CHUNK)
     flags = [here == before] + [here == at(m) for m in (1, 2, 3)]
-    return here, [here.astype(F32)] + [f.astype(F32) for f in flags]
-
-
-def scatter_sum(parts, axis):
-    low = parts.astype(BF16)
-    out = lax.psum_scatter(low, "shard", scatter_dimension=axis, tiled=True)
-    return lax.psum(out, "ctx").astype(F32)
+    return jnp.stack([here.astype(F32)] + [f.astype(F32) for f in flags], axis=1)
 
 
 def shards(
@@ -516,151 +1153,136 @@
     dv = conv_value.shape[2] * shard_size
     sizes = (heads, dk, dv)
     gather = lambda v, axis: lax.all_gather(v, "shard", axis=axis, tiled=True)
-    mixer_w = gather(jnp.concatenate([w_query, w_key, w_value, w_outgate], axis=1), 0)
-    mlp_w = gather(jnp.concatenate([w_gate, w_up], axis=1), 0)
-    out_w = gather(w_out, 1)
-    down_w = gather(w_down, 1)
-    tiny = [norm_gain, mlp_gain, w_beta, w_decay, conv_query, conv_key, conv_value, out_gain]
+    spare = jnp.zeros((w_beta.shape[0], 128 - 2 * heads), BF16)
+    mixer_w = gather(
+        jnp.concatenate([w_query, w_key, w_value, w_outgate, w_beta, w_decay, spare], axis=1), 0
+    )
+    tiny = [norm_gain, mlp_gain, conv_query, conv_key, conv_value, out_gain]
     flat = jnp.concatenate([v.reshape(-1) for v in tiny])
     flat = lax.all_gather(flat, "shard", axis=0)
+    out_w = gather(w_out, 1)
+    gate_w = gather(w_gate, 0)
+    up_w = gather(w_up, 0)
+    down_w = gather(w_down, 1)
     cuts, at = [], 0
     for v in tiny:
         cuts.append(flat[:, at : at + v.size].reshape((shard_size,) + v.shape))
         at += v.size
-    gain_one = cuts[0].reshape(-1).astype(F32)
-    gain_two = cuts[1].reshape(-1).astype(F32)
-    small_w = jnp.concatenate([cuts[2], cuts[3]], axis=2).reshape(model, 2 * heads)
-    taps = [jnp.moveaxis(c, 0, 2).reshape(c.shape[1], -1) for c in cuts[4:7]]
+    gain_one = cuts[0].reshape(1, -1).astype(F32)
+    gain_two = cuts[1].reshape(1, -1).astype(F32)
+    taps = [jnp.moveaxis(c, 0, 2).reshape(c.shape[1], -1) for c in cuts[2:5]]
     taps = jnp.concatenate(taps, axis=1).astype(F32)
-    head_gain = jnp.moveaxis(cuts[7], 0, 1).reshape(heads, dv).astype(F32)
+    head_gain = jnp.moveaxis(cuts[5], 0, 1).reshape(1, heads * dv).astype(F32)
     conv_width = taps.shape[1]
-
-    here, facts = row_facts(segment_ids, ctx_rank * rows_here, rows_here)
-    live_rows = (here >= 0).astype(F32)
+    facts = row_facts(segment_ids, ctx_rank * rows_here, rows_here)
+    bias = jnp.zeros((1, 128), F32)
+    bias = lax.dynamic_update_slice(bias, decay_bias.astype(F32)[None], (0, heads))
+
     inputs32 = tokens.astype(F32)
-    normed32, norm_one_back = jax.vjp(rms_norm, inputs32, gain_one)
-    normed = normed32.astype(BF16)
+    normed = (normalise(inputs32)[0] * gain_one).astype(BF16)
     raw = dot_plain(normed, mixer_w[:, :conv_width]).astype(BF16)
-    gate_raw = dot_plain(normed, mixer_w[:, conv_width:])
-    small_lin = dot_plain(normed, small_w)
-    (beta_rows, decays), rates_back = jax.vjp(
-        gate_rates, small_lin[:, :heads], small_lin[:, heads:], decay_bias.astype(F32)
-    )
-    low = lambda v: v.astype(BF16).astype(F32)
-    columns = [low(beta_rows)[:, h] for h in range(heads)]
-    columns += [low(decays)[:, h] for h in range(heads)] + facts
-    columns += [jnp.zeros((rows_here,), F32)] * (16 - len(columns))
-    aux = jnp.stack(columns, axis=1)
+    gates = dot_plain(normed, mixer_w[:, conv_width:])
     ahead = [(i, i + 1) for i in range(ctx_size - 1)]
     behind = [(i + 1, i) for i in range(ctx_size - 1)]
     halo = lax.ppermute(raw[rows_here - 8 :], "ctx", ahead)
-    unit, val, inv, wu, mix, just, total = prepare(sizes, raw, halo, aux, taps)
+    unit, val, inv, wu, mix, just, total, aux = prepare(
+        sizes, raw, halo, gates, bias, facts, taps
+    )
     start = lax.ppermute(total, "ctx", ahead)
     for _ in range(ctx_size - 2):
         start = lax.ppermute(apply_states(sizes, mix, wu, aux, start)[2], "ctx", ahead)
-    mixed, states, _ = apply_states(sizes, mix, wu, aux, start)
-
-    gated32, gated_back = jax.vjp(
-        lambda mixed_in, gate_in, gain_in: gated_norm(mixed_in, gate_in, gain_in, live_rows),
-        mixed.astype(F32), gate_raw, head_gain,
-    )
-    gated_rows = gated32.astype(BF16)
-    attended = lax.psum(dot_plain(gated_rows, out_w).astype(BF16), "tp").astype(F32)
-    hidden_in = inputs32 + attended
-    normed_two32, norm_two_back = jax.vjp(rms_norm, hidden_in, gain_two)
-    normed_two = normed_two32.astype(BF16)
-    both_two = dot_plain(normed_two, mlp_w)
-    units = w_gate.shape[1]
-    gate_two, up_two = both_two[:, :units], both_two[:, units:]
+    mixed, states, gated, hidden_in, normed_two = out_sum(
+        sizes, mix, wu, aux, start, gates, head_gain, out_w, tokens, gain_two
+    )
+
+    gate_two = dot_plain(normed_two, gate_w)
+    up_two = dot_plain(normed_two, up_w)
     sigmoid_two = jax.nn.sigmoid(gate_two)
     activated = gate_two * sigmoid_two
     hidden = (activated * up_two).astype(BF16)
-    mlp_out = lax.psum(dot_plain(hidden, down_w).astype(BF16), "tp").astype(F32)
-    result = (hidden_in + mlp_out).astype(BF16)
     grad_hidden = dot_back(cotangent, down_w)
     gate_slope = sigmoid_two * (1.0 + gate_two * (1.0 - sigmoid_two))
     grad_gate = (grad_hidden * up_two * gate_slope).astype(BF16)
     grad_up = (grad_hidden * activated).astype(BF16)
-    grad_both = jnp.concatenate([grad_gate, grad_up], axis=1)
-    part_mlp = scatter_sum(dot_outer(normed_two, grad_both), 0)
-    part_down = scatter_sum(dot_outer(hidden, cotangent), 1)
-    grad_normed_two = lax.psum(dot_back(grad_both, mlp_w).astype(BF16), "tp").astype(F32)
-    grad_hidden_in, grad_gain_two = norm_two_back(grad_normed_two)
-    grad_hidden_in = grad_hidden_in + cotangent.astype(F32)
-    grad_branch = grad_hidden_in.astype(BF16)
-    part_out = scatter_sum(dot_outer(gated_rows, grad_branch), 1)
-    grad_gated = dot_back(grad_branch, out_w)
-    grad_mixed, grad_gate_raw, grad_head_gain = gated_back(grad_gated)
-    grad_mixed = grad_mixed.astype(BF16)
-    zero = jnp.zeros((heads, dk, dv), F32)
-    end = lax.ppermute(back_chain(sizes, mix, grad_mixed, aux, zero), "ctx", behind)
+    mlp_part = dot_plain(hidden, down_w).astype(BF16)
+    mlp_parts = [
+        dot_outer(normed_two, grad_gate),
+        dot_outer(normed_two, grad_up),
+        dot_outer(hidden, cotangent),
+    ]
+    found = mlp_back_sum(
+        sizes, grad_gate, grad_up, gate_w, up_w, hidden_in, cotangent, mixed, gates, aux, mix,
+        out_w, head_gain, gain_two, mlp_parts, (0, 0, 1),
+    )
+    gh, branch, grad_mixed, grad_gate_low, chain, grad_gain_two, grad_head_gain = found[:7]
+    part_gate, part_up, part_down = found[7:]
+    mlp_part, gh = lax.optimization_barrier((mlp_part, gh))
+    mlp_out = lax.psum(mlp_part, "tp")
+    result = (hidden_in + mlp_out.astype(F32)).astype(BF16)
+    end = lax.ppermute(chain, "ctx", behind)
     for _ in range(ctx_size - 2):
         end = lax.ppermute(back_chain(sizes, mix, grad_mixed, aux, end), "ctx", behind)
-    draw, tail, head, dtaps, daux = back_states(
+    draw, tail, head, dtaps, dsmall, dbias = back_states(
         sizes, raw, halo, aux, taps, unit, val, inv, wu, mix, just, states, grad_mixed, end
     )
     tail = (tail + lax.ppermute(head, "ctx", behind)).astype(BF16)
     draw = lax.dynamic_update_slice(draw, tail, (rows_here - 8, 0))
-    grad_gate_low = grad_gate_raw.astype(BF16)
-    grad_beta_lin, grad_decay_lin, grad_bias = rates_back(
-        (daux[:, :heads], daux[:, heads : 2 * heads])
-    )
-    grad_small = jnp.concatenate([grad_beta_lin, grad_decay_lin], axis=1).astype(BF16)
-    grad_mix = jnp.concatenate([draw, grad_gate_low], axis=1)
-    grad_mixer_w = dot_outer(normed, grad_mix)
-    grad_small_w = dot_outer(normed, grad_small)
-    grad_normed_part = dot_back(grad_mix, mixer_w) + dot_back(grad_small, small_w)
-    grad_normed = lax.psum(grad_normed_part.astype(BF16), "tp").astype(F32)
-    grad_inputs, grad_gain_one = norm_one_back(grad_normed)
-    input_grad = grad_inputs + grad_hidden_in
-    part_mixer = scatter_sum(grad_mixer_w, 0)
-    split = lambda v: v.reshape(shard_size, -1)
     taps_parts = []
     first = 0
     for width in (heads * dk, heads * dk, heads * dv):
         part = dtaps[:4, first : first + width].reshape(4, heads, shard_size, -1)
         taps_parts.append(jnp.moveaxis(part, 2, 0))
         first += width
+    lines = lambda v: v.reshape(shard_size, -1, 128)
+    bias_row = jnp.broadcast_to(dbias[0:1][None], (shard_size, 1, 128))
     tiny_grads = [
-        split(grad_gain_one), split(grad_gain_two), split(grad_small_w),
-        split(jnp.broadcast_to(grad_bias[None], (shard_size, heads))),
-        *[split(p) for p in taps_parts],
-        split(jnp.moveaxis(grad_head_gain.reshape(heads, shard_size, -1), 1, 0)),
+        jnp.zeros((shard_size, norm_gain.shape[0] // 128, 128), F32), lines(grad_gain_two[0]),
+        bias_row, *[lines(p) for p in taps_parts],
+        lines(jnp.moveaxis(grad_head_gain[0].reshape(heads, shard_size, -1), 1, 0)),
     ]
+    tiny_grads = jnp.concatenate(tiny_grads, axis=1)
+    tiny_grads = jnp.pad(tiny_grads, ((0, 0), (0, -tiny_grads.shape[1] % 8), (0, 0)))
+    mixer_parts = [
+        dot_outer(normed, draw), dot_outer(normed, grad_gate_low), dot_outer(normed, dsmall),
+        dot_outer(gated, branch),
+    ]
+    qw, vw = heads * dk, heads * dv
+    found = mixer_back_sum(
+        sizes, draw, grad_gate_low, dsmall, mixer_w, tokens, gh, gain_one, tiny_grads,
+        mixer_parts, (0, 0, 0, 1),
+        ((qw, qw, vw), (vw,), (128,), (model // shard_size,)),
+    )
+    input_grad, mine, part_query, part_key, part_value, part_outgate, part_small, part_out = found
     shapes = [
-        norm_gain.shape, mlp_gain.shape, (w_beta.shape[0], 2 * heads), decay_bias.shape,
-        conv_query.shape, conv_key.shape, conv_value.shape, out_gain.shape,
+        norm_gain.shape, mlp_gain.shape, (128,), conv_query.shape, conv_key.shape,
+        conv_value.shape, out_gain.shape,
     ]
-    packed = jnp.concatenate(tiny_grads, axis=1)
-    packed = lax.psum(packed, ("shard", "ctx"))
-    mine = lax.dynamic_slice_in_dim(packed, lax.axis_index("shard"), 1, 0)[0]
     small, at = [], 0
     for shape in shapes:
         count = 1
         for n in shape:
             count *= n
-        small.append(mine[at : at + count].reshape(shape))
-        at += count
-    qw, vw = heads * dk, heads * dv
+        small.append(mine[at : at + count // 128].reshape(shape))
+        at += count // 128
     return (
         result,
         input_grad,
         small[0],
-        part_mixer[:, :qw],
-        part_mixer[:, qw : 2 * qw],
-        part_mixer[:, 2 * qw : 2 * qw + vw],
-        part_mixer[:, 2 * qw + vw :],
-        small[2][:, :heads],
-        small[2][:, heads:],
+        part_query,
+        part_key,
+        part_value,
+        part_outgate,
+        part_small[:, :heads],
+        part_small[:, heads : 2 * heads],
+        small[2][heads : 2 * heads],
         small[3],
         small[4],
         small[5],
         small[6],
-        small[7],
         part_out,
         small[1],
-        part_mlp[:, :units],
-        part_mlp[:, units:],
+        part_gate,
+        part_up,
         part_down,
     )
 

time: 767 us -> 449 us (0.59)
  waiting for transfers between devices: 433 us -> 18.7 us
  Pallas kernels: 70 us -> 286 us
  other arithmetic: 50.3 us -> 7.58 us
  blocking collectives: 33.4 us -> 6.25 us
  matrix products: 78.4 us -> 56.3 us
  local copies, waits for them, and re-layouts: 61 us -> 43 us
  starting transfers between devices: 18.6 us -> 7.64 us
    psum x4 -> x1, waiting for transfers between devices: 344 us -> 0.01 us  [shards(): mlp_out = lax.psum(mlp_part, 'tp')]
    pallas_call x2 -> x3, Pallas kernels: 13.2 us -> 224 us  [the longest x1 84.3 us: mixer_back_sum(): pl.pallas_call(functools.partial(mixer_back_kernel, sizes, blocks, axes,...]
    all_gather x4 -> x5, waiting for transfers between devices: 54.5 us -> 15.9 us  [shards(): gather = lambda v, axis: lax.all_gather(v, 'shard', axis=axis, tiled=True)]
    reduce_sum x7 -> x1, other arithmetic: 29.7 us -> 0.48 us  [normalise(): rate = lax.rsqrt(jnp.mean(vector * vector, axis=1, keepdims=True) + EPSILON)]
    psum x1 -> x0, blocking collectives: 27.2 us -> none  [shards(): packed = lax.psum(packed, ('shard', 'ctx'))]
    dot_general x5 -> x1, matrix products: 26 us -> 4.85 us  [dot_back(): return lax.dot_general(left, right, NT, preferred_element_type=F32)]
    reduce_scatter x4 -> x0, waiting for transfers between devices: 18.9 us -> none  [scatter_sum(): out = lax.psum_scatter(low, 'shard', scatter_dimension=axis, tiled=True)]
    another operation x9 -> x4, local copies, waits for them, and re-layouts: 11.5 us -> 1.16 us  [the longest x2 1.07 us: row_facts(): jnp.stack([here.astype(F32)] + [f.astype(F32) for f in flags], axis=1)]
  transfers between devices with their start and end apart: 16 -> 10, of which waited for: 10 -> 2; matrix products, arithmetic and copies ran while one was open for 20% -> 14% of each run, Pallas kernels for 9% -> 48%
where the time goes in v2:
time: 449 us; the launch traced here: 440 us
  Pallas kernels  286 us (64%)
  matrix products  56.3 us (13%)
  local copies, waits for them, and re-layouts  43 us (10%)
  waiting for transfers between devices  18.7 us (4%)
  between operations  15 us (3%)
  starting transfers between devices  7.64 us (2%)
  other arithmetic  7.58 us (2%)
  blocking collectives  6.25 us (1%)
    pallas_call x1, Pallas kernels, mixer_back_sum(): pl.pallas_call(functools.partial(mixer_back_kernel, sizes, blocks, axes,...  84.3 us
    pallas_call x1, Pallas kernels, mlp_back_sum(): pl.pallas_call(functools.partial(mlp_back_kernel, sizes, blocks, axes), g...  75.7 us
    pallas_call x1, Pallas kernels, out_sum(): pl.pallas_call(functools.partial(out_kernel, sizes, blocks), grid=(blocks...  64.4 us
    pallas_call x1, Pallas kernels, back_states(): pl.pallas_call(functools.partial(back_kernel, sizes), grid=(blocks,), in_...  35.5 us
    dot_general x5, matrix products, dot_plain(): return jnp.dot(left, right, preferred_element_type=F32)  25.9 us
    pallas_call x1, Pallas kernels, prepare(): pl.pallas_call(functools.partial(prepare_kernel, sizes), grid=(blocks,),...  25.6 us
    dot_general x7, matrix products, dot_outer(): lax.dot_general(left, right, TN, preferred_element_type=F32).astype(BF16)  25.5 us
    unnamed x93, local copies, waits for them, and re-layouts  21.6 us
  transfers between devices with their start and end apart: 10, of which 2 were waited for; matrix products, arithmetic and copies ran while one was open for 14% of the time, Pallas kernels for 48%

profile of v2, /device:TPU:0, one launch (start us, length us, event | category | flops | bytes accessed | tf_op | source)
XLA Modules:
  0.0 440.0 jit_solution(16840105735248854804)
XLA Ops:
  8.9 2.1 concatenate.23
  16.3 6.2 %all-gather.1 = bf16[4,1,1664]{2,1,0:T(2,128)(2,1)S(1)} all-gather(bf16[1,1,1664]{2,1,0:T(2,128)(2,1)S(1)} %reshape.212), channel_id=2, replica_groups=mesh['shard'=4,'ctx'=2,'tp'=4] {'shard'}, dimensions={0}, use_global_device_ids=true | all-gather | bytes 16640 | tf_op jit(solution)/shard_map/all_gather | solution.py:1162
  28.2 15.8 %all-gather.8.cloned.1.call-done.refs_3_ = bf16[1024,1664]{1,0:T(8,128)(2,1)} async-done(((bf16[256,1664]{1,0:T(8,128)(2,1)}), bf16[1024,1664]{1,0:T(8,128)(2,1)}) %all-gather.8.cloned.1.call-update) | async-done | bytes 3407888 | tf_op jit(solution)/shard_map/all_gather | solution.py:1155
  44.0 4.0 fusion.6.raw_ref.prev_ref
  48.0 3.4 collective-permute-start
  51.4 4.7 %fusion.9.lin_ref.gate_ref.refs_7_ = f32[1024,640]{1,0:T(8,128)} fusion(bf16[1024,1664]{1,0:T(8,128)(2,1)} %all-gather.8.cloned.1.call-done.refs_3_, bf16[1024,1024]{1,0:T(8,128)(2,1)S(1)} %copy-done.2, f32[1024]{0:T(1024)S(1)} %bitcast.105, f32[1024]{0:T(1024)S(1)} %add_rsqrt_fusion), kind=kOutput, calls=%fused_computation.21 | convolution fusion | flops 1346371584 | bytes 6037504 | tf_op jit(solution)/shard_map/dot_general | solution.py:1117
  56.8 25.6 %delta_prepare.1 = (bf16[1024,512]{1,0:T(8,128)(2,1)}, bf16[1024,512]{1,0:T(8,128)(2,1)}, bf16[1024,256]{1,0:T(8,128)(2,1)}, bf16[1024,768]{1,0:T(8,128)(2,1)}, ...) custom-call(bf16[1024,1024]{1,0:T(8,128)(2,1)} %copy-done, ...), custom_call_target="tpu_custom_call" | custom-call | tf_op jit(solution)/shard_map/delta_prepare/pallas_call | solution.py:168
  82.4 1.3 collective-permute-start.1
  83.7 4.9 %fusion.27 = f32[1024,704]{1,0:T(8,128)} fusion(bf16[1024,1024]{1,0:T(8,128)(2,1)S(1)} %copy-done.4, bf16[704,1024]{1,0:T(8,128)(2,1)} %all-gather.16.cloned.1.call-done), kind=kOutput, calls=%fused_computation.65 | convolution fusion | flops 1476395008 | bytes 6422528 | tf_op jit(solution)/shard_map/dot_general | solution.py:1121
  88.6 1.3 collective-permute-done.1.start_ref
  90.7 64.4 %out_sum.1 = (bf16[1024,512]{1,0:T(8,128)(2,1)}, bf16[8,2,128,256]{3,2,1,0:T(8,128)(2,1)}, bf16[1024,512]{1,0:T(8,128)(2,1)}, f32[1024,1024]{1,0:T(8,128)}, bf16[1024,1024]{1,0:T(8,128)(2,1)}) custom-call(bf16[8,2,256,256]{3,2,1,0:T(8,128)(2,1)} %get-tuple-element.58.mix_ref.refs_9_, bf16[1024,768]{1,0:T(8,128)(2,1)} %get-tuple-element.59.wu_ref, ...), custom_call_target="tpu_custom_call" | custom-call | flops 4000000000 | bytes 150000000 | tf_op jit(solution)/shard_map/out_sum/pallas_call | solution.py:801
  155.1 5.5 %fusion.26 = f32[1024,704]{1,0:T(8,128)} fusion(bf16[1024,1024]{1,0:T(8,128)(2,1)} %get-tuple-element.63, bf16[1024,704]{1,0:T(8,128)(2,1)} %all-gather.14.cloned.1.call-done.refs_3_), kind=kOutput, calls=%fused_computation.64 | convolution fusion | flops 1476395008 | bytes 6422528 | tf_op jit(solution)/shard_map/dot_general | solution.py:1117
  160.6 8.6 %multiply_convert_fusion = (bf16[1024,704]{1,0:T(8,128)(2,1)}, bf16[1024,704]{1,0:T(8,128)(2,1)S(1)}, bf16[1024,704]{1,0:T(8,128)(2,1)}) fusion(f32[1024,704]{1,0:T(8,128)} %fusion.27, f32[1024,704]{1,0:T(8,128)} %fusion.26, bf16[1024,1024]{1,0:T(8,128)(2,1)} %get-tuple-element.63, bf16[1024,704]{1,0:T(8,128)(2,1)} %all-gather.12.cloned.1.call-done.refs_2_), kind=kOutput, calls=%fused_computation.6 | convolution fusion | flops 1487208448 | bytes 13631488 | tf_op jit(solution)/shard_map/dot_general | solution.py:1117
  170.3 1.7 convolution_convert_fusion.4
  172.0 1.6 copy.192.refs_13_
  173.6 3.7 convolution_convert_fusion.3
  177.3 1.6 copy.193.refs_14_
  178.9 4.3 convolution_convert_fusion.2.refs_15_
  183.3 3.1 convolution_convert_fusion.1
  186.4 75.7 %mlp_back_sum.1 = (f32[1024,1024]{1,0:T(8,128)}, bf16[1024,1024]{1,0:T(8,128)(2,1)}, bf16[1024,512]{1,0:T(8,128)(2,1)}, bf16[1024,512]{1,0:T(8,128)(2,1)}, f32[2...) custom-call(bf16[1024,704]{1,0:T(8,128)(2,1)} %copy-done.5, ...), custom_call_target="tpu_custom_call" | custom-call | flops 6000000000 | bytes 150000000 | tf_op jit(solution)/shard_map/mlp_back_sum/pallas_call | solution.py:944
  262.2 1.4 collective-permute-start.2
  265.3 3.7 convolution_convert_fusion.6.refs_9_
  269.0 2.3 copy.200
  271.4 2.2 copy.201
  273.6 3.8 convolution_convert_fusion.5.refs_11_
  278.2 35.5 %delta_back.1 = (bf16[1024,1024]{1,0:T(8,128)(2,1)}, f32[8,1024]{1,0:T(8,128)}, f32[8,1024]{1,0:T(8,128)}, f32[8,1024]{1,0:T(8,128)}, bf16[1024,128]{1,0:T(8,128)(2,1)}, /*index=5*/f32[8,128]{1,0:T(8,128)}) custom-call(bf16[1024,1024]{1,0:T(8,128)(2,1)} %copy-done, bf16[1024,1024]{1,0:T(8,128)(2,1)} %copy-done, bf16[8,1024]{1,0:T(8,128)(2,1)} %copy-done.17, ...), custom_call_target="tpu_custom_call" | custom-call | tf_op jit(solution)/shard_map/delta_back/pallas_call | solution.py:456
  315.7 2.7 convolution_convert_fusion.7.refs_10_
  322.0 5.5 %convolution_convert_fusion.refs_8_ = bf16[1024,1024]{1,0:T(8,128)(2,1)} fusion(bf16[1024,1024]{1,0:T(8,128)(2,1)} %fusion.11.refs_0_, bf16[1024,1024]{1,0:T(8,128)(2,1)S(1)} %copy-done.3, f32[1024]{0:T(1024)S(1)} %bitcast.108, f32[1024]{0:T(1024)S(1)} %copy-done.22), kind=kOutput, calls=%fused_computation.14 | convolution fusion | flops 2152726528 | bytes 6299648 | tf_op jit(solution)/shard_map/dot_general | solution.py:1125
  327.5 84.3 %mixer_back_sum.1 = (f32[1024,1024]{1,0:T(8,128)}, f32[16,128]{1,0:T(8,128)}, f32[256,256]{1,0:T(8,128)}, f32[256,256]{1,0:T(8,128)}, f32[256,512]{1,0:T(8,128)}...) custom-call(bf16[1024,1024]{1,0:T(8,128)(2,1)} %fusion.11.refs_0_, ...), custom_call_target="tpu_custom_call" | custom-call | flops 6000000000 | bytes 150000000 | tf_op jit(solution)/shard_map/mixer_back_sum/pallas_call | solution.py:1087
  414.9 1.4 slice_bitcast_fusion
  420.9 5.1 %add_convert_fusion = bf16[1024,1024]{1,0:T(8,128)(2,1)} fusion(f32[1024,1024]{1,0:T(8,128)} %get-tuple-element.62.refs_4_, bf16[1024,1024]{1,0:T(8,128)(2,1)} %all-reduce.6.cloned.1.call-done), kind=kLoop, calls=%fused_computation.5 | loop fusion | flops 3145728 | bytes 8388608 | tf_op jit(solution)/shard_map/convert_element_type | solution.py:1221
  426.1 2.0 copy.242
  (174 shorter events, 35.3 us)
Async XLA Ops:
  7.2 5.5 %copy-start.11 = (bf16[256,704]{0,1:T(8,128)(2,1)S(1)}, bf16[256,704]{0,1:T(8,128)(2,1)}, u32[]{:S(2)}) copy-start(bf16[256,704]{0,1:T(8,128)(2,1)} %param.38) | copy-start | bytes 1081348
  7.2 36.8 %all-gather.8.cloned.1.call-start = ((), (), s32[]{:S(2)}) async-start(), calls=%async_computation | async-start | bytes 4259840 | tf_op jit(solution)/shard_map/all_gather | solution.py:1155
  8.9 4.8 %copy-start.12 = (bf16[256,704]{0,1:T(8,128)(2,1)S(1)}, bf16[256,704]{0,1:T(8,128)(2,1)}, u32[]{:S(2)}) copy-start(bf16[256,704]{0,1:T(8,128)(2,1)} %param.37) | copy-start | bytes 1081348
  11.1 3.6 copy-start.23
  11.1 3.7 copy-start.24
  11.1 3.8 copy-start.25
  11.1 3.9 copy-start.30
  11.1 4.0 copy-start.26
  11.1 4.2 copy-start.27
  11.1 11.5 %copy-start.2 = (bf16[1024,1024]{1,0:T(8,128)(2,1)S(1)}, bf16[1024,1024]{1,0:T(8,128)(2,1)}, u32[]{:S(2)}) copy-start(bf16[1024,1024]{1,0:T(8,128)(2,1)} %refs_4_.1) | copy-start | bytes 6291460
  11.2 72.6 %all-gather.16.cloned.1.call-start = ((), (), s32[]{:S(2)}) async-start(), calls=%async_computation.4 | async-start | bytes 1802240 | tf_op jit(solution)/shard_map/all_gather | solution.py:1155
  11.9 76.7 %all-gather.10.cloned.1.call-start = ((), (), s32[]{:S(2)}) async-start(), calls=%async_computation.1 | async-start | bytes 1310720 | tf_op jit(solution)/shard_map/all_gather | solution.py:1155
  12.6 142.4 %all-gather.14.cloned.1.call-start = ((), (), s32[]{:S(2)}) async-start(), calls=%async_computation.3 | async-start | bytes 1966080 | tf_op jit(solution)/shard_map/all_gather | solution.py:1155
  13.6 9.5 %copy-start.31 = (bf16[2]{0:T(256)(128)(2,1)S(1)}, bf16[2]{0:T(256)(128)(2,1)}, u32[]{:S(2)}) copy-start(bf16[2]{0:T(256)(128)(2,1)} %param.30) | copy-start | bytes 16
  13.6 10.1 %copy-start.16 = (s32[2048]{0:T(1024)S(1)}, s32[2048]{0:T(1024)}, u32[]{:S(2)}) copy-start(s32[2048]{0:T(1024)} %param.21) | copy-start | bytes 24580
  13.6 147.0 %all-gather.12.cloned.1.call-start = ((), (), s32[]{:S(2)}) async-start(), calls=%async_computation.2 | async-start | bytes 1966080 | tf_op jit(solution)/shard_map/all_gather | solution.py:1155
  14.6 406.3 %all-reduce.6.cloned.1.call-start = ((), (), s32[]{:S(2)}) async-start(), calls=%async_computation.5 | async-start | bytes 4194304 | tf_op jit(solution)/shard_map/psum | solution.py:1220
  22.6 28.8 %copy-start.19 = (f32[1,2,4,128]{3,1,2,0:T(2,128)}, f32[1,2,4,128]{3,1,2,0:T(2,128)S(1)}, u32[]{:S(2)}) copy-start(f32[1,2,4,128]{3,1,2,0:T(2,128)S(1)} %copy.206) | copy-start | bytes 12292
  23.1 28.3 %copy-start.21 = (f32[1024]{0:T(1024)}, f32[1024]{0:T(1024)S(1)}, u32[]{:S(2)}) copy-start(f32[1024]{0:T(1024)S(1)} %add_rsqrt_fusion) | copy-start | bytes 12292
  48.0 8.2 %copy-start = (bf16[1024,1024]{1,0:T(8,128)(2,1)}, bf16[1024,1024]{1,0:T(8,128)(2,1)S(1)}, u32[]{:S(2)}) copy-start(bf16[1024,1024]{1,0:T(8,128)(2,1)S(1)} %fusion.6.raw_ref.prev_ref) | copy-start | bytes 6291460
  48.0 8.1 %collective-permute-start = (bf16[8,1024]{1,0:T(8,128)(2,1)S(1)}, bf16[8,1024]{1,0:T(8,128)(2,1)S(1)}, u32[]{:S(2)}, u32[]{:S(2)}) collective-permute-start(bf16[8,1024]{1,0:T(8,128)(2,1)S(1)} %slice.121), channel_id=1, source_target_pairs={{0,4},{1,5},{2,6},{3,7},{8,12},{9,13},{10,14},{11,15},{16,20},{17,... | collective-permute-start | bytes 49160 | tf_op jit(solution)/shard_map/ppermute | solution.py:1187
  56.2 27.6 %copy-start.4 = (bf16[1024,1024]{1,0:T(8,128)(2,1)S(1)}, bf16[1024,1024]{1,0:T(8,128)(2,1)}, u32[]{:S(2)}) copy-start(bf16[1024,1024]{1,0:T(8,128)(2,1)} %refs_5_.1) | copy-start | bytes 6291460
  82.4 7.6 %collective-permute-start.1 = (f32[2,128,256]{2,1,0:T(8,128)}, f32[2,128,256]{2,1,0:T(8,128)S(1)}, u32[]{:S(2)}, u32[]{:S(2)}) collective-permute-start(f32[2,128,256]{2,1,0:T(8,128)} %get-tuple-element.61), channel_id=1, source_target_pairs={{0,4},{1,5},{2,6},{3,7},{8,12},{9,13},{10,14},{11,15},{16,20},{17,... | collective-permute-start | bytes 786440 | tf_op jit(solution)/shard_map/ppermute | solution.py:1191
  160.6 9.7 %copy-start.32 = (bf16[1024,1024]{1,0:T(8,128)(2,1)S(1)}, bf16[1024,1024]{1,0:T(8,128)(2,1)}, u32[]{:S(2)}) copy-start(bf16[1024,1024]{1,0:T(8,128)(2,1)} %get-tuple-element.63) | copy-start | bytes 6291460
  178.9 4.3 copy-start.28
  178.9 4.3 copy-start.33
  262.2 15.3 %collective-permute-start.2 = (f32[2,128,256]{2,1,0:T(8,128)}, f32[2,128,256]{2,1,0:T(8,128)S(1)}, u32[]{:S(2)}, u32[]{:S(2)}) collective-permute-start(f32[2,128,256]{2,1,0:T(8,128)} %get-tuple-element.73), channel_id=1, source_target_pairs={{4,0},{5,1},{6,2},{7,3},{12,8},{13,9},{14,10},{15,11},{20,16},{21,... | collective-permute-start | bytes 786440 | tf_op jit(solution)/shard_map/ppermute | solution.py:1222
  269.0 4.6 %copy-start.6 = (bf16[1024,512]{1,0:T(8,128)(2,1)S(1)}, bf16[1024,512]{1,0:T(8,128)(2,1)}, u32[]{:S(2)}) copy-start(bf16[1024,512]{1,0:T(8,128)(2,1)} %get-tuple-element.84) | copy-start | bytes 3145732
  313.7 7.7 %collective-permute-start.3 = (f32[8,1024]{1,0:T(8,128)}, f32[8,1024]{1,0:T(8,128)S(1)}, u32[]{:S(2)}, u32[]{:S(2)}) collective-permute-start(f32[8,1024]{1,0:T(8,128)} %get-tuple-element.76), channel_id=1, source_target_pairs={{4,0},{5,1},{6,2},{7,3},{12,8},{13,9},{14,10},{15,11},{20,16},{21,... | collective-permute-start | bytes 98312 | tf_op jit(solution)/shard_map/ppermute | solution.py:1228
  315.7 5.7 %copy-start.18 = (f32[8,1024]{1,0:T(8,128)S(1)}, f32[8,1024]{1,0:T(8,128)}, u32[]{:S(2)}) copy-start(f32[8,1024]{1,0:T(8,128)} %get-tuple-element.75) | copy-start | bytes 98308
  420.9 5.1 %copy-start.1 = (f32[1024,1024]{1,0:T(8,128)S(1)}, f32[1024,1024]{1,0:T(8,128)}, u32[]{:S(2)}) copy-start(f32[1024,1024]{1,0:T(8,128)} %get-tuple-element.251) | copy-start | bytes 12582916
  428.1 3.8 copy-start.7
  (12 other events, 26.1 us)
Sparse Core Ops, SparseCore 0:
  11.3 32.7 all-gather.7
  45.6 19.0 all-gather.15
  66.3 16.8 all-gather.9
  85.2 19.5 all-gather.13
  106.8 19.6 all-gather.11
  262.3 86.8 all-reduce.5
